TPU v7x, 256 devices: a whole 4x4x8 slice. The times are simulated.
256 devices in a mesh: row: 16 (over x_hi, y, core), col: 16 (over x_lo, z).
Axes of the slice: x: 4 (x_hi: 2, x_lo: 2; x = x_hi * 2 + x_lo), y: 4, z: 8, core: 2. Of those that a mesh axis runs over, the one named last changes fastest.
Arguments:
- object_field: float32 [2, 6144, 6144], P(None, 'row', 'col'), may hold values from -4 to 4
- illumination: float32 [2, 256, 256], replicated, may hold values from -4 to 4
- measured: float32 [16, 16, 8, 256, 256], P('row', 'col'), may hold values from 0.05 to 4
- positions: int32 [16, 16, 8, 2], P('row', 'col'), may hold values from 0 to 383
- frame_counts: int32 [16, 16], P('row', 'col'), may hold values from 1 to 8, as said below
- first_count: int32 [16, 16], P('row', 'col'), may hold values from 0 to 4
Outputs:
- new_object: float32 [2, 6144, 6144], P(None, 'row', 'col')
- new_illumination: float32 [2, 256, 256], replicated
Inputs may be any that keep to these rules, and one draw needn't show every extreme that they name: `frame_counts`: some tile has exactly 8 live frames in every draw; slots from a tile's count on are unused.
All inputs are finite; a program needn't handle non-finite values.
Results may differ from a plain program's by a relative error of at most 0.0003.
Values sent between devices are 32-bit elements; how exact they have to be, the bound alone decides.
A program may use at most 64 MiB of HBM per device.

v0:
```python
import functools
import math

import jax
import jax.numpy as jnp
import numpy as np
from jax import lax
from jax.experimental import pallas as pl
from jax.experimental.pallas import tpu as pltpu
from jax.sharding import PartitionSpec as P

MESH = pl.DeviceIdType.MESH
TILE, PROBE, EXT = 384, 256, 640
N_ROW = N_COL = 16
F32, BF16 = jnp.float32, jnp.bfloat16
VMEM_SPEC = pl.BlockSpec(memory_space=pltpu.VMEM)
SMEM_SPEC = pl.BlockSpec(memory_space=pltpu.SMEM)
ANY_SPEC = pl.BlockSpec(memory_space=pl.ANY)


def split_bf16(table):
    high = table.astype(np.float32).astype(BF16)
    low = (table - high.astype(np.float64)).astype(np.float32).astype(BF16)
    return high, low


def dft_tables():
    n = np.arange(128)[:, None]
    parts = []
    for parity in (0, 1):
        k = 2 * np.arange(128)[None, :] + parity
        angle = ((n * k) % 256) * (2.0 * np.pi / 256.0)
        c, s = np.cos(angle) / 16.0, np.sin(angle) / 16.0
        table = np.block([[c, -s], [s, c]])
        parts.append((split_bf16(table), split_bf16(table.T)))
    order = []
    for transposed in (0, 1):
        for parity in (0, 1):
            order.extend(parts[parity][transposed])
    return np.stack(order)


def deinterleave_table():
    table = np.zeros((256, 256), np.float32)
    index = np.arange(128)
    table[2 * index, index] = 1.0
    table[2 * index + 1, 128 + index] = 1.0
    return table.astype(BF16)


def place():
    row, col = lax.axis_index("row"), lax.axis_index("col")
    return row, col


def remote(src, dst, send_sem, recv_sem, device):
    return pltpu.make_async_remote_copy(
        src_ref=src, dst_ref=dst, send_sem=send_sem, recv_sem=recv_sem,
        device_id=device, device_id_type=MESH,
    )


def greet_neighbours(barrier, row, col):
    for has, device in (
        (row > 0, (row - 1, col)),
        (row < N_ROW - 1, (row + 1, col)),
        (col > 0, (row, col - 1)),
        (col < N_COL - 1, (row, col + 1)),
    ):
        @pl.when(has)
        def _(device=device):
            pl.semaphore_signal(barrier, inc=1, device_id=device, device_id_type=MESH)


def neighbour_count(row, col):
    one, none = jnp.int32(1), jnp.int32(0)
    has = (row > 0, row < N_ROW - 1, col > 0, col < N_COL - 1)
    return sum(jnp.where(h, one, none) for h in has)


LEFT_CHUNKS = ((0, 0, 256), (1, 0, 256), (0, 256, 128), (1, 256, 128))


class Halo:
    def __init__(self, ext, left_sems, up_sems, corner_sems, row, col):
        self.ext, self.row, self.col = ext, row, col
        self.left_sems, self.up_sems, self.corner_sems = left_sems, up_sems, corner_sems

    def left(self, index):
        channel, start, rows = LEFT_CHUNKS[index]
        return remote(
            self.ext.at[channel, pl.ds(0, 2), pl.ds(start, rows), :],
            self.ext.at[channel, pl.ds(3, 2), pl.ds(start, rows), :],
            self.left_sems.at[0, index], self.left_sems.at[1, index],
            (self.row, jnp.maximum(self.col - 1, 0)),
        )

    def up(self, channel):
        return remote(
            self.ext.at[channel, pl.ds(0, 3), pl.ds(0, 256), :],
            self.ext.at[channel, pl.ds(0, 3), pl.ds(384, 256), :],
            self.up_sems.at[0, channel], self.up_sems.at[1, channel],
            (jnp.maximum(self.row - 1, 0), self.col),
        )

    def corner(self, channel):
        return remote(
            self.ext.at[channel, pl.ds(3, 2), pl.ds(0, 256), :],
            self.ext.at[channel, pl.ds(3, 2), pl.ds(384, 256), :],
            self.corner_sems.at[0, channel], self.corner_sems.at[1, channel],
            (jnp.maximum(self.row - 1, 0), self.col),
        )

    def clear_edges(self):
        @pl.when(self.col == N_COL - 1)
        def _():
            for channel in range(2):
                for block in (3, 4):
                    self.ext[channel, block] = jnp.zeros((EXT, 128), F32)

        @pl.when(self.row == N_ROW - 1)
        def _():
            for channel in range(2):
                for block in range(5):
                    self.ext[channel, block, 384:640] = jnp.zeros((256, 128), F32)

    @property
    def sends_left(self):
        return self.col > 0

    @property
    def sends_up(self):
        return self.row > 0

    @property
    def takes_right(self):
        return self.col < N_COL - 1

    @property
    def takes_below(self):
        return self.row < N_ROW - 1

    def forward_corner(self, channel):
        @pl.when(self.takes_right)
        def _():
            self.left(channel).wait_recv()

            @pl.when(self.sends_up)
            def _():
                self.corner(channel).start()

    def finish(self):
        for index in range(4):
            @pl.when(self.sends_left)
            def _(index=index):
                self.left(index).wait_send()

        for index in (2, 3):
            @pl.when(self.takes_right)
            def _(index=index):
                self.left(index).wait_recv()

        for channel in range(2):
            @pl.when(self.sends_up)
            def _(channel=channel):
                self.up(channel).wait_send()

                @pl.when(self.takes_right)
                def _():
                    self.corner(channel).wait_send()

            @pl.when(self.takes_below)
            def _(channel=channel):
                self.up(channel).wait_recv()

                @pl.when(self.takes_right)
                def _():
                    self.corner(channel).wait_recv()


def fetch_kernel(object_ref, measured_ref, order_ref, ext_ref, sorted_ref,
                 turned, load_sems, left_sems, up_sems, corner_sems):
    row, col = place()
    barrier = pltpu.get_barrier_semaphore()
    greet_neighbours(barrier, row, col)
    loads = []
    for channel in range(2):
        for block in range(3):
            load = pltpu.make_async_copy(
                object_ref.at[channel, :, pl.ds(block * 128, 128)],
                ext_ref.at[channel, block, pl.ds(0, TILE), :],
                load_sems.at[channel * 3 + block],
            )
            load.start()
            loads.append(load)
    halo = Halo(ext_ref, left_sems, up_sems, corner_sems, row, col)
    halo.clear_edges()
    for load in loads:
        load.wait()
    pl.semaphore_wait(barrier, neighbour_count(row, col))

    @pl.when(halo.sends_left)
    def _():
        for index in range(4):
            halo.left(index).start()

    @pl.when(halo.sends_up)
    def _():
        for channel in range(2):
            halo.up(channel).start()

    def sort_frame(frame, carry):
        value = measured_ref[frame]
        total = jnp.zeros((256, 256), F32)
        for _ in range(3):
            piece = value.astype(BF16)
            value = value - piece.astype(F32)
            total = total + jnp.dot(piece, order_ref[...], preferred_element_type=F32)
        for block in range(2):
            turned[block] = total[:, block * 128:block * 128 + 128]
        for block in range(2):
            for parity in range(2):
                sorted_ref[frame, parity, :, block * 128:block * 128 + 128] = (
                    turned[block, pl.ds(parity, 128, stride=2), :])
        return carry

    lax.fori_loop(0, measured_ref.shape[0], sort_frame, 0)
    for channel in range(2):
        halo.forward_corner(channel)
    halo.finish()


def fetch(object_field, measured, order):
    dma = pltpu.SemaphoreType.DMA
    frames = measured.shape[0]
    return pl.pallas_call(
        fetch_kernel,
        name="fetch",
        out_shape=(
            jax.ShapeDtypeStruct((2, 5, EXT, 128), F32),
            jax.ShapeDtypeStruct((frames, 2, 128, 256), F32),
        ),
        in_specs=[ANY_SPEC, VMEM_SPEC, VMEM_SPEC],
        out_specs=(VMEM_SPEC, VMEM_SPEC),
        scratch_shapes=[
            pltpu.VMEM((2, 256, 128), F32), dma((6,)), dma((2, 4)), dma((2, 2)), dma((2, 2))],
        compiler_params=pltpu.CompilerParams(collective_id=0, has_side_effects=True),
    )(object_field, measured, order)


def halves(value):
    high = value.astype(BF16)
    low = (value - high.astype(F32)).astype(BF16)
    return high, low


def dot(left, right):
    return jnp.dot(left, right, preferred_element_type=F32)


def times_table(value, tables, index):
    high, low = halves(value)
    return dot(high, tables[index]) + dot(low, tables[index]) + dot(high, tables[index + 1])


def table_times(tables, index, value):
    high, low = halves(value)
    return dot(tables[index], high) + dot(tables[index + 1], high) + dot(tables[index], low)


def beside(a, b):
    return jnp.concatenate([a, b], axis=1)


def above(a, b):
    return jnp.concatenate([a, b], axis=0)


def frames_kernel(batch, counts_ref, first_ref, positions_ref, ext_ref, probe_ref, sorted_ref,
                  tables, grad_ref, probe_grad_ref):
    live = counts_ref[0, 0]
    first = jnp.minimum(first_ref[0, 0], live)
    start, end = (0, first) if batch == 0 else (first, live)
    for channel in range(2):
        for block in range(5):
            grad_ref[channel, block] = jnp.zeros((EXT, 128), F32)
    probe_grad_ref[...] = jnp.zeros_like(probe_grad_ref)
    lanes = lax.broadcasted_iota(jnp.int32, (256, 128), 1)

    def add_frame(frame, carry):
        row_start = positions_ref[frame, 0]
        col_start = positions_ref[frame, 1]
        block0 = col_start // 128
        shift = col_start - block0 * 128
        rows = pl.ds(row_start, 256)
        back_shift = jnp.bitwise_and(128 - shift, 127)

        window = []
        for channel in range(2):
            turned = [
                pltpu.roll(ext_ref[channel, block0 + block, rows, :], back_shift, 1)
                for block in range(3)
            ]
            keep = lanes < 128 - shift
            window.append([jnp.where(keep, turned[b], turned[b + 1]) for b in range(2)])
        probe = [[probe_ref[channel * 512 + b * 256: channel * 512 + b * 256 + 256, :]
                  for b in range(2)] for channel in range(2)]
        exit_re = [probe[0][b] * window[0][b] - probe[1][b] * window[1][b] for b in range(2)]
        exit_im = [probe[0][b] * window[1][b] + probe[1][b] * window[0][b] for b in range(2)]
        y0 = times_table(beside(exit_re[0] + exit_re[1], exit_im[0] + exit_im[1]), tables, 0)
        y1 = times_table(beside(exit_re[0] - exit_re[1], exit_im[0] - exit_im[1]), tables, 2)

        def stacked(t0, t1):
            return above(beside(t0[:, :128], t1[:, :128]), beside(t0[:, 128:], t1[:, 128:]))

        w0 = table_times(tables, 4, stacked(y0[:128] + y0[128:], y1[:128] + y1[128:]))
        w1 = table_times(tables, 6, stacked(y0[:128] - y0[128:], y1[:128] - y1[128:]))

        def weighted(w, parity):
            re, im = w[:128], w[128:]
            residue = re * re + im * im - sorted_ref[frame, parity]
            return above(residue * re, residue * im)

        u0 = table_times(tables, 0, weighted(w0, 0))
        u1 = table_times(tables, 2, weighted(w1, 1))
        top, bottom = u0 + u1, u0 - u1
        z_re = above(top[:128], bottom[:128])
        z_im = above(top[128:], bottom[128:])
        v0 = times_table(beside(z_re[:, :128], z_im[:, :128]), tables, 4)
        v1 = times_table(beside(z_re[:, 128:], z_im[:, 128:]), tables, 6)
        back_re = [v0[:, :128] + v1[:, :128], v0[:, :128] - v1[:, :128]]
        back_im = [v0[:, 128:] + v1[:, 128:], v0[:, 128:] - v1[:, 128:]]

        for b in range(2):
            r0 = b * 256
            probe_grad_ref[r0:r0 + 256, :] += window[0][b] * back_re[b] + window[1][b] * back_im[b]
            probe_grad_ref[512 + r0:768 + r0, :] += (
                window[0][b] * back_im[b] - window[1][b] * back_re[b])
        before = lanes < shift
        zero = jnp.zeros((256, 128), F32)
        for channel in range(2):
            if channel == 0:
                term = [probe[0][b] * back_re[b] + probe[1][b] * back_im[b] for b in range(2)]
            else:
                term = [probe[0][b] * back_im[b] - probe[1][b] * back_re[b] for b in range(2)]
            turned = [pltpu.roll(term[b], shift, 1) for b in range(2)]
            adds = [
                jnp.where(before, zero, turned[0]),
                jnp.where(before, turned[0], turned[1]),
                jnp.where(before, turned[1], zero),
            ]
            for block in range(3):
                at = (channel, block0 + block, rows, slice(None))
                grad_ref[at] = grad_ref[at] + adds[block]
        return carry

    lax.fori_loop(start, end, add_frame, 0)


def frames(batch, counts, first, positions, ext, probe, ordered, tables):
    return pl.pallas_call(
        functools.partial(frames_kernel, batch),
        name=f"frames{batch}",
        out_shape=(
            jax.ShapeDtypeStruct((2, 5, EXT, 128), F32),
            jax.ShapeDtypeStruct((1024, 128), F32),
        ),
        in_specs=[SMEM_SPEC, SMEM_SPEC, SMEM_SPEC] + [VMEM_SPEC] * 4,
        out_specs=(VMEM_SPEC, VMEM_SPEC),
    )(counts, first, positions, ext, probe, ordered, tables)


class Reduce:
    def __init__(self, grad, half, quarter, piece, got_half, got_quarter, got_piece, got_z,
                 full, sums, sems, row, col):
        self.grad, self.half, self.quarter, self.piece = grad, half, quarter, piece
        self.got_half, self.got_quarter = got_half, got_quarter
        self.got_piece, self.got_z = got_piece, got_z
        self.full, self.sums, self.sems = full, sums, sems
        self.row, self.col = row, col
        self.core = row % 2
        self.y = (row % 8) // 2
        self.x = (row // 8) * 2 + col // 8
        self.z = col % 8

    def partner(self):
        return (self.row + 1 - 2 * self.core, self.col)

    def x_peer(self, step):
        x = (self.x + step) % 4
        return x, ((x // 2) * 8 + self.row % 8, (x % 2) * 8 + self.z)

    def y_peer(self, step):
        y = (self.y + step) % 4
        return y, ((self.row // 8) * 8 + y * 2 + self.core, self.col)

    def z_peer(self, step):
        z = (self.z + step) % 8
        return z, (self.row, (self.col // 8) * 8 + z)

    def peers(self):
        found = [self.partner()]
        found += [self.x_peer(step)[1] for step in range(1, 4)]
        found += [self.y_peer(step)[1] for step in range(1, 4)]
        found += [self.z_peer(step)[1] for step in range(1, 8)]
        return found

    def copy(self, src, dst, index, device):
        return remote(src, dst, self.sems.at[0, index], self.sems.at[1, index], device)

    def pair(self):
        other = pl.multiple_of((1 - self.core) * 512, 512)
        return self.copy(self.grad.at[pl.ds(other, 512), :], self.got_half, 0, self.partner())

    def over_x(self, step):
        x, device = self.x_peer(step)
        return self.copy(self.half.at[pl.ds(pl.multiple_of(x * 128, 128), 128), :],
                         self.got_quarter.at[step - 1], step, device)

    def over_y(self, step):
        y, device = self.y_peer(step)
        return self.copy(self.quarter.at[pl.ds(pl.multiple_of(y * 32, 32), 32), :],
                         self.got_piece.at[step - 1], 3 + step, device)

    def over_z(self, step):
        _, device = self.z_peer(step)
        return self.copy(self.piece, self.got_z.at[self.z], 6 + step, device)

    def back_y(self, step):
        _, device = self.y_peer(step)
        mine = self.sums.at[pl.ds(pl.multiple_of(self.full_at(), 32), 32), :]
        return self.copy(mine, mine, 13 + step, device)

    def back_x(self, step):
        _, device = self.x_peer(step)
        mine = self.sums.at[pl.ds(pl.multiple_of(self.core * 512 + self.x * 128, 128), 128), :]
        return self.copy(mine, mine, 16 + step, device)

    def back_pair(self):
        mine = self.sums.at[pl.ds(pl.multiple_of(self.core * 512, 512), 512), :]
        return self.copy(mine, mine, 20, self.partner())

    def full_at(self):
        return self.core * 512 + self.x * 128 + self.y * 32

    def stages(self):
        def begin():
            self.pair().start()

        def to_x():
            self.pair().wait_recv()
            mine = pl.multiple_of(self.core * 512, 512)
            self.half[...] = self.grad[pl.ds(mine, 512), :] + self.got_half[...]
            for step in range(1, 4):
                self.over_x(step).start()

        def to_y():
            for step in range(1, 4):
                self.over_x(step).wait_recv()
            mine = pl.multiple_of(self.x * 128, 128)
            self.quarter[...] = (self.half[pl.ds(mine, 128), :] + self.got_quarter[0]) + (
                self.got_quarter[1] + self.got_quarter[2])
            for step in range(1, 4):
                self.over_y(step).start()

        def to_z():
            for step in range(1, 4):
                self.over_y(step).wait_recv()
            mine = pl.multiple_of(self.y * 32, 32)
            self.piece[...] = (self.quarter[pl.ds(mine, 32), :] + self.got_piece[0]) + (
                self.got_piece[1] + self.got_piece[2])
            for step in range(1, 8):
                self.over_z(step).start()
            self.got_z[self.z] = self.piece[...]

        def from_z():
            for step in range(1, 8):
                z = (self.z + 8 - step) % 8
                self.copy(self.piece, self.got_z.at[z], 6 + step, self.z_peer(step)[1]).wait_recv()
            total = self.got_z[0]
            for z in range(1, 8):
                total = total + self.got_z[z]
            self.sums[pl.ds(pl.multiple_of(self.full_at(), 32), 32), :] = total
            for step in range(1, 4):
                self.back_y(step).start()

        def from_y():
            for step in range(1, 4):
                y = (self.y + 4 - step) % 4
                at = pl.multiple_of(self.core * 512 + self.x * 128 + y * 32, 32)
                theirs = self.sums.at[pl.ds(at, 32), :]
                self.copy(theirs, theirs, 13 + step, self.y_peer(step)[1]).wait_recv()
            for step in range(1, 4):
                self.back_x(step).start()

        def from_x():
            for step in range(1, 4):
                x = (self.x + 4 - step) % 4
                at = pl.multiple_of(self.core * 512 + x * 128, 128)
                theirs = self.sums.at[pl.ds(at, 128), :]
                self.copy(theirs, theirs, 16 + step, self.x_peer(step)[1]).wait_recv()
            self.back_pair().start()

        def end():
            at = pl.multiple_of((1 - self.core) * 512, 512)
            theirs = self.sums.at[pl.ds(at, 512), :]
            self.copy(theirs, theirs, 20, self.partner()).wait_recv()
            self.pair().wait_send()
            for step in range(1, 4):
                self.over_x(step).wait_send()
                self.over_y(step).wait_send()
                self.back_x(step).wait_send()
                self.back_y(step).wait_send()
            for step in range(1, 8):
                self.over_z(step).wait_send()
            self.back_pair().wait_send()

        return begin, to_x, to_y, to_z, from_z, from_y, from_x, end


RIGHT_CHUNKS = ((0, 256, 128), (1, 256, 128), (0, 0, 256), (1, 0, 256))


def exchange_kernel(refetch, object_ref, grad_ref, probe_ref, probe_grad_ref, out_ref, probe_out,
                    from_above, from_left, joined,
                    half, quarter, piece, got_half, got_quarter, got_piece, got_z, sums,
                    down_sems, right_sems, reduce_sems, *halo_sems):
    row, col = place()
    reduce = Reduce(probe_grad_ref, half, quarter, piece, got_half, got_quarter, got_piece, got_z,
                    None, sums, reduce_sems, row, col)
    begin, to_x, to_y, to_z, from_z, from_y, from_x, end = reduce.stages()
    barrier = pltpu.get_barrier_semaphore()
    greet_neighbours(barrier, row, col)
    for device in reduce.peers():
        pl.semaphore_signal(barrier, inc=1, device_id=device, device_id_type=MESH)
    sends_down, takes_above = row < N_ROW - 1, row > 0
    sends_right, takes_left = col < N_COL - 1, col > 0
    if refetch:
        halo = Halo(out_ref, *halo_sems, row, col)
        halo.clear_edges()

    @pl.when(row == 0)
    def _():
        for channel in range(2):
            for block in range(5):
                from_above[channel, block] = jnp.zeros((256, 128), F32)

    @pl.when(col == 0)
    def _():
        for channel in range(2):
            for block in range(2):
                from_left[channel, block] = jnp.zeros((TILE, 128), F32)

    pl.semaphore_wait(barrier, 14 + neighbour_count(row, col))

    def down(channel, part):
        blocks = pl.ds(3, 2) if part == 0 else pl.ds(0, 3)
        return remote(
            grad_ref.at[channel, blocks, pl.ds(384, 256), :],
            from_above.at[channel, blocks, :, :],
            down_sems.at[0, channel, part], down_sems.at[1, channel, part],
            (jnp.minimum(row + 1, N_ROW - 1), col),
        )

    def right(index):
        channel, start, rows = RIGHT_CHUNKS[index]
        if index < 2:
            source = grad_ref.at[channel, pl.ds(3, 2), pl.ds(start, rows), :]
        else:
            source = joined.at[channel]
        return remote(
            source, from_left.at[channel, :, pl.ds(start, rows), :],
            right_sems.at[0, index], right_sems.at[1, index],
            (row, jnp.minimum(col + 1, N_COL - 1)),
        )

    begin()

    @pl.when(sends_right)
    def _():
        right(0).start()
        right(1).start()

    @pl.when(sends_down)
    def _():
        for part in range(2):
            for channel in range(2):
                down(channel, part).start()

    def take_above(channel, part):
        @pl.when(takes_above)
        def _():
            down(channel, part).wait_recv()

    def join(channel):
        take_above(channel, 0)
        for block in range(2):
            joined[channel, block] = (
                grad_ref[channel, 3 + block, 0:256] + from_above[channel, 3 + block])

        @pl.when(sends_right)
        def _():
            right(2 + channel).start()

    def take_left(index):
        @pl.when(takes_left)
        def _():
            right(index).wait_recv()

    def put(channel, block, start, rows, value):
        if refetch:
            out_ref[channel, block, start:start + rows] = value
        else:
            out_ref[channel, start:start + rows, block * 128:block * 128 + 128] = value

    def update_low(channel):
        rows = slice(256, 384)
        for block in range(3):
            grad = grad_ref[channel, block, rows]
            if block < 2:
                grad = grad + from_left[channel, block, rows]
            put(channel, block, 256, 128, object_ref[channel, block, rows] - 0.1 * grad)

    def update_top(channel):
        rows = slice(0, 256)
        for block in range(3):
            grad = grad_ref[channel, block, rows] + from_above[channel, block]
            if block < 2:
                grad = grad + from_left[channel, block, rows]
            put(channel, block, 0, 256, object_ref[channel, block, rows] - 0.1 * grad)

    def send_left(index):
        if refetch:
            @pl.when(halo.sends_left)
            def _():
                halo.left(index).start()

    def send_up(channel):
        if refetch:
            @pl.when(halo.sends_up)
            def _():
                halo.up(channel).start()

    to_x()
    join(0)
    to_y()
    join(1)
    for channel in range(2):
        take_left(channel)
        update_low(channel)
        send_left(2 + channel)
    to_z()
    take_above(0, 1)
    take_left(2)
    update_top(0)
    send_left(0)
    send_up(0)
    from_z()
    take_above(1, 1)
    from_y()
    take_left(3)
    update_top(1)
    send_left(1)
    send_up(1)
    from_x()
    if refetch:
        halo.forward_corner(0)
    end()
    step_size = 0.5 / math.sqrt(N_ROW * N_COL * 8)
    probe_out[...] = probe_ref[...] - step_size * sums[...]
    if refetch:
        halo.forward_corner(1)
        halo.finish()

    @pl.when(sends_down)
    def _():
        for part in range(2):
            for channel in range(2):
                down(channel, part).wait_send()

    @pl.when(sends_right)
    def _():
        for index in range(4):
            right(index).wait_send()


def exchange(refetch, ext, grad, probe, probe_grad):
    dma = pltpu.SemaphoreType.DMA
    out = (2, 5, EXT, 128) if refetch else (2, TILE, TILE)
    halo_sems = [dma((2, 4)), dma((2, 2)), dma((2, 2))] if refetch else []
    return pl.pallas_call(
        functools.partial(exchange_kernel, refetch),
        name=f"exchange{int(refetch)}",
        out_shape=(jax.ShapeDtypeStruct(out, F32), jax.ShapeDtypeStruct((1024, 128), F32)),
        in_specs=[VMEM_SPEC] * 4,
        out_specs=(VMEM_SPEC, VMEM_SPEC),
        scratch_shapes=[
            pltpu.VMEM((2, 5, 256, 128), F32),
            pltpu.VMEM((2, 2, TILE, 128), F32),
            pltpu.VMEM((2, 2, 256, 128), F32),
            pltpu.VMEM((512, 128), F32),
            pltpu.VMEM((128, 128), F32),
            pltpu.VMEM((32, 128), F32),
            pltpu.VMEM((512, 128), F32),
            pltpu.VMEM((3, 128, 128), F32),
            pltpu.VMEM((3, 32, 128), F32),
            pltpu.VMEM((8, 32, 128), F32),
            pltpu.VMEM((1024, 128), F32),
            dma((2, 2, 2)),
            dma((2, 4)),
            dma((2, 21)),
        ] + halo_sems,
        compiler_params=pltpu.CompilerParams(
            collective_id=1 + int(refetch), has_side_effects=True),
    )(ext, grad, probe, probe_grad)


def to_blocks(probe):
    return probe.reshape(2, 256, 2, 128).transpose(0, 2, 1, 3).reshape(1024, 128)


def from_blocks(blocks):
    return blocks.reshape(2, 2, 256, 128).transpose(0, 2, 1, 3).reshape(2, 256, 256)


def per_device(object_field, illumination, measured, positions, frame_counts, first_count):
    tables = jnp.asarray(dft_tables())
    order = jnp.asarray(deinterleave_table())
    positions = positions[0, 0]
    probe = to_blocks(illumination)
    ext, ordered = fetch(object_field, measured[0, 0], order)
    grad, probe_grad = frames(
        0, frame_counts, first_count, positions, ext, probe, ordered, tables)
    ext, probe = exchange(True, ext, grad, probe, probe_grad)
    grad, probe_grad = frames(
        1, frame_counts, first_count, positions, ext, probe, ordered, tables)
    new_object, probe = exchange(False, ext, grad, probe, probe_grad)
    return new_object, from_blocks(probe)


def solution(mesh):
    in_specs = (
        P(None, "row", "col"),
        P(),
        P("row", "col", None, None, None),
        P("row", "col", None, None),
        P("row", "col"),
        P("row", "col"),
    )
    out_specs = (P(None, "row", "col"), P())
    return jax.shard_map(
        per_device, mesh=mesh, in_specs=in_specs, out_specs=out_specs, check_vma=False
    )
```

profile of v0, /device:TPU:1, one launch (start us, length us, event | category | flops | bytes accessed | tf_op | source)
XLA Modules:
  0.0 188.2 jit_solution(12764451035521143874)
XLA Ops:
  0.6 0.0 copy-start
  2.0 1.3 copy.11.positions_ref
  3.3 0.0 copy-done
  3.3 0.8 copy_bitcast_fusion.1
  4.2 27.5 %fetch.1 = (f32[2,5,640,128]{3,2,1,0:T(8,128)}, f32[8,2,128,256]{3,2,1,0:T(8,128)}) custom-call(f32[2,384,384]{2,1,0:T(8,128)} %object_ref.1, f32[8,256,256]{2,1,0:T(8,128)} %bitcast.19, bf16[256,256]{1,0:T(8,128)(2,1)} %constant.5.clone.order_ref), custom_call_target="tpu_custom_call" | custom-call | tf_op jit(solution)/shard_map/fetch/pallas_call | solution.py:236
  31.7 8.8 %frames0.1 = (f32[2,5,640,128]{3,2,1,0:T(8,128)}, f32[1024,128]{1,0:T(8,128)}) custom-call(s32[1,1]{1,0:T(1,128)S(6)} %copy.20.counts_ref, s32[1,1]{1,0:T(1,128)S(6)} %copy.21.first_ref, s32[8,2]{1,0:T(8,128)} %copy.11.positions_ref, f32[2,5,640,128]{3,2,1,0:T(8,128)} %get-tuple-element.12.ext_ref.object_ref, f32[1024,128]{1,0:T(8,128)} %bitcast.17, ...), custom_call_target="tpu_custom_call" | custom-call | tf_op jit(solution)/shard_map/frames0/pallas_call | solution.py:361
  40.5 70.8 %exchange1.1 = (f32[2,5,640,128]{3,2,1,0:T(8,128)}, f32[1024,128]{1,0:T(8,128)}) custom-call(f32[2,5,640,128]{3,2,1,0:T(8,128)} %get-tuple-element.12.ext_ref.object_ref, f32[2,5,640,128]{3,2,1,0:T(8,128)} %get-tuple-element.14.grad_ref, f32[1024,128]{1,0:T(8,128)} %bitcast.18, f32[1024,128]{1,0:T(8,128)} %get-tuple-element.15.probe_grad_ref), custom_call_target="tpu_custom_call" | custom-call | tf_op jit(solution)/shard_map/exchange1/pallas_call | solution.py:691
  111.3 5.1 %frames1.1 = (f32[2,5,640,128]{3,2,1,0:T(8,128)}, f32[1024,128]{1,0:T(8,128)}) custom-call(s32[1,1]{1,0:T(1,128)S(6)} %copy.20.counts_ref, s32[1,1]{1,0:T(1,128)S(6)} %copy.21.first_ref, s32[8,2]{1,0:T(8,128)} %copy.11.positions_ref, f32[2,5,640,128]{3,2,1,0:T(8,128)} %get-tuple-element.16.ext_ref.object_ref, f32[1024,128]{1,0:T(8,128)} %get-tuple-element.17.probe_ref, ...), custom_call_target="tpu_custom_call" | custom-call | tf_op jit(solution)/shard_map/frames1/pallas_call | solution.py:361
  116.5 67.4 %exchange0.1 = (f32[2,384,384]{2,1,0:T(8,128)}, f32[1024,128]{1,0:T(8,128)}) custom-call(f32[2,5,640,128]{3,2,1,0:T(8,128)} %get-tuple-element.16.ext_ref.object_ref, f32[2,5,640,128]{3,2,1,0:T(8,128)} %get-tuple-element.18.grad_ref, f32[1024,128]{1,0:T(8,128)} %get-tuple-element.17.probe_ref, f32[1024,128]{1,0:T(8,128)} %get-tuple-element.19.probe_grad_ref), custom_call_target="tpu_custom_call" | custom-call | tf_op jit(solution)/shard_map/exchange0/pallas_call | solution.py:691
  183.9 1.9 copy.18
  185.8 2.4 %copy.22 = f32[2,384,384]{2,1,0:T(8,128)} copy(f32[2,384,384]{2,1,0:T(8,128)} %get-tuple-element.24) | data formatting | bytes 2359296
Async XLA Ops:
  0.6 2.7 %copy-start = (f32[2,256,256]{2,1,0:T(8,128)S(1)}, f32[2,256,256]{2,1,0:T(8,128)}, u32[]{:S(2)}) copy-start(f32[2,256,256]{2,1,0:T(8,128)} %param.9) | copy-start | bytes 1572868
where the time goes:
time: 187 us; the launch traced here: 188 us
  Pallas kernels  180 us (96%)
  local copies, waits for them, and re-layouts  6.42 us (3%)
  between operations  2.01 us (1%)
    pallas_call x2, Pallas kernels, exchange(): pl.pallas_call(functools.partial(exchange_kernel, refetch), name=f'exchan...  138 us
    pallas_call x1, Pallas kernels, fetch(): pl.pallas_call(fetch_kernel, name='fetch', out_shape=(jax.ShapeDtypeStruc...  27.5 us
    pallas_call x2, Pallas kernels, frames(): pl.pallas_call(functools.partial(frames_kernel, batch), name=f'frames{bat...  14 us

commit v1 on v0

v1 whole, which is shorter than its diff:
```python
import functools
import math

import jax
import jax.numpy as jnp
import numpy as np
from jax import lax
from jax.experimental import pallas as pl
from jax.experimental.pallas import tpu as pltpu
from jax.sharding import PartitionSpec as P

MESH = pl.DeviceIdType.MESH
TILE, PROBE, EXT = 384, 256, 640
N_ROW = N_COL = 16
F32, BF16 = jnp.float32, jnp.bfloat16
FETCH_VMEM, FRAMES_VMEM, EXCHANGE_VMEM = 14 << 20, 16 << 20, 18 << 20
VMEM_SPEC = pl.BlockSpec(memory_space=pltpu.VMEM)
SMEM_SPEC = pl.BlockSpec(memory_space=pltpu.SMEM)
HBM_SPEC = pl.BlockSpec(memory_space=pltpu.HBM)


def split_bf16(table):
    high = table.astype(np.float32).astype(BF16)
    low = (table - high.astype(np.float64)).astype(np.float32).astype(BF16)
    return high, low


def dft_tables():
    n = np.arange(128)[:, None]
    parts = []
    for parity in (0, 1):
        k = 2 * np.arange(128)[None, :] + parity
        angle = ((n * k) % 256) * (2.0 * np.pi / 256.0)
        c, s = np.cos(angle) / 16.0, np.sin(angle) / 16.0
        table = np.block([[c, -s], [s, c]])
        parts.append((split_bf16(table), split_bf16(table.T)))
    order = []
    for transposed in (0, 1):
        for parity in (0, 1):
            order.extend(parts[parity][transposed])
    return np.stack(order)


def deinterleave_table():
    table = np.zeros((256, 256), np.float32)
    index = np.arange(128)
    table[2 * index, index] = 1.0
    table[2 * index + 1, 128 + index] = 1.0
    return table.astype(BF16)


def place():
    row, col = lax.axis_index("row"), lax.axis_index("col")
    return row, col


def remote(src, dst, send_sem, recv_sem, device):
    return pltpu.make_async_remote_copy(
        src_ref=src, dst_ref=dst, send_sem=send_sem, recv_sem=recv_sem,
        device_id=device, device_id_type=MESH,
    )


UP_DETOUR = ((8, 15), (14, 15), (6, 7), (7, 15))
DOWN_DETOUR = ((7, 0), (1, 0), (9, 8), (8, 0))


def is_at(row, col, device):
    return (row == device[0]) & (col == device[1])


def place_of(device):
    return jnp.int32(device[0]), jnp.int32(device[1])


def greet_detour(barrier, row, col, detour):
    for hop in range(3):
        for here, there in ((detour[hop], detour[hop + 1]), (detour[hop + 1], detour[hop])):
            @pl.when(is_at(row, col, here))
            def _(there=there):
                pl.semaphore_signal(
                    barrier, inc=1, device_id=place_of(there), device_id_type=MESH)


def detour_count(row, col, detour):
    one, two, none = jnp.int32(1), jnp.int32(2), jnp.int32(0)
    ends = is_at(row, col, detour[0]) | is_at(row, col, detour[3])
    middles = is_at(row, col, detour[1]) | is_at(row, col, detour[2])
    return jnp.where(ends, one, none) + jnp.where(middles, two, none)


def greet_neighbours(barrier, row, col):
    for has, device in (
        (row > 0, (row - 1, col)),
        (row < N_ROW - 1, (row + 1, col)),
        (col > 0, (row, col - 1)),
        (col < N_COL - 1, (row, col + 1)),
    ):
        @pl.when(has)
        def _(device=device):
            pl.semaphore_signal(barrier, inc=1, device_id=device, device_id_type=MESH)


def neighbour_count(row, col):
    one, none = jnp.int32(1), jnp.int32(0)
    has = (row > 0, row < N_ROW - 1, col > 0, col < N_COL - 1)
    return sum(jnp.where(h, one, none) for h in has)


CHUNKS = ((0, 64), (64, 64), (128, 64), (192, 64), (256, 64), (320, 64))
TOPS = 4
LOWS = (4, 5)
EVERY = 6


class Halo:
    def __init__(self, ext, detour, left_sems, up_sems, corner_sems, detour_sems, row, col):
        self.ext, self.row, self.col = ext, row, col
        self.left_sems, self.up_sems, self.corner_sems = left_sems, up_sems, corner_sems
        self.detour, self.detour_sems = detour, detour_sems
        self.stops = [is_at(row, col, UP_DETOUR[hop]) for hop in range(3)]
        self.sends_left, self.takes_right = col > 0, col < N_COL - 1
        self.sends_up, self.takes_below = row > 0, row < N_ROW - 1
        self.sends_direct = self.sends_up & jnp.logical_not(self.stops[0])

    def left(self, index):
        start, rows = CHUNKS[index]
        return remote(
            self.ext.at[:, pl.ds(0, 2), pl.ds(start, rows), :],
            self.ext.at[:, pl.ds(3, 2), pl.ds(start, rows), :],
            self.left_sems.at[0, index], self.left_sems.at[1, index],
            (self.row, jnp.maximum(self.col - 1, 0)),
        )

    def over(self, index, blocks, sems):
        start, rows = CHUNKS[index]
        return remote(
            self.ext.at[:, blocks, pl.ds(start, rows), :],
            self.ext.at[:, blocks, pl.ds(384 + start, rows), :],
            sems.at[0, index], sems.at[1, index],
            (jnp.maximum(self.row - 1, 0), self.col),
        )

    def up(self, index):
        return self.over(index, pl.ds(0, 3), self.up_sems)

    def corner(self, index):
        return self.over(index, pl.ds(3, 2), self.corner_sems)

    def detour_hop(self, hop, index):
        start, rows = CHUNKS[index]
        first, last = hop == 0, hop == 2
        source = self.ext if first else self.detour
        target = self.ext.at[:, pl.ds(0, 3), pl.ds(384 + start, rows), :] if last else (
            self.detour.at[:, :, pl.ds(start, rows), :])
        return remote(
            source.at[:, pl.ds(0, 3), pl.ds(start, rows), :], target,
            self.detour_sems.at[0, index],
            self.up_sems.at[1, index] if last else self.detour_sems.at[1, index],
            place_of(UP_DETOUR[hop + 1]),
        )

    def pass_on(self, index):
        for hop in (1, 2):
            @pl.when(self.stops[hop])
            def _(hop=hop):
                self.detour_hop(hop - 1, index).wait_recv()
                self.detour_hop(hop, index).start()

    def clear_edges(self):
        @pl.when(self.col == N_COL - 1)
        def _():
            for channel in range(2):
                for block in (3, 4):
                    self.ext[channel, block] = jnp.zeros((EXT, 128), F32)

        @pl.when(self.row == N_ROW - 1)
        def _():
            for channel in range(2):
                for block in range(5):
                    self.ext[channel, block, 384:640] = jnp.zeros((256, 128), F32)

    def send_left(self, index):
        @pl.when(self.sends_left)
        def _():
            self.left(index).start()

    def send_up(self, index):
        @pl.when(self.sends_direct)
        def _():
            self.up(index).start()

        @pl.when(self.stops[0])
        def _():
            self.detour_hop(0, index).start()

    def forward_corner(self, index):
        @pl.when(self.takes_right)
        def _():
            self.left(index).wait_recv()

            @pl.when(self.sends_up)
            def _():
                self.corner(index).start()

    def finish(self):
        @pl.when(self.takes_right)
        def _():
            for index in LOWS:
                self.left(index).wait_recv()

        @pl.when(self.takes_below)
        def _():
            for index in range(TOPS):
                self.up(index).wait_recv()

        @pl.when(self.takes_below & self.takes_right)
        def _():
            for index in range(TOPS):
                self.corner(index).wait_recv()

        @pl.when(self.sends_left)
        def _():
            for index in range(EVERY):
                self.left(index).wait_send()

        @pl.when(self.sends_direct)
        def _():
            for index in range(TOPS):
                self.up(index).wait_send()

        for hop in range(3):
            @pl.when(self.stops[hop])
            def _(hop=hop):
                for index in range(TOPS):
                    self.detour_hop(hop, index).wait_send()

        @pl.when(self.sends_up & self.takes_right)
        def _():
            for index in range(TOPS):
                self.corner(index).wait_send()


def halo_sems():
    dma = pltpu.SemaphoreType.DMA
    return [pltpu.VMEM((2, 3, 256, 128), F32), dma((2, EVERY)), dma((2, TOPS)), dma((2, TOPS)),
            dma((2, TOPS))]


def fetch_kernel(object_ref, measured_ref, order_ref, ext_ref, sorted_ref,
                 turned, measured, load_sems, *sems):
    row, col = place()
    barrier = pltpu.get_barrier_semaphore()
    greet_neighbours(barrier, row, col)
    greet_detour(barrier, row, col, UP_DETOUR)
    loads = []
    for channel in range(2):
        for block in range(3):
            load = pltpu.make_async_copy(
                object_ref.at[channel, :, pl.ds(block * 128, 128)],
                ext_ref.at[channel, block, pl.ds(0, TILE), :],
                load_sems.at[channel * 3 + block],
            )
            load.start()
            loads.append(load)
    load_frames = pltpu.make_async_copy(measured_ref, measured, load_sems.at[6])
    load_frames.start()
    halo = Halo(ext_ref, *sems, row, col)
    halo.clear_edges()
    for load in loads:
        load.wait()
    pl.semaphore_wait(barrier, neighbour_count(row, col) + detour_count(row, col, UP_DETOUR))
    for index in range(EVERY):
        halo.send_left(index)
    for index in range(TOPS):
        halo.send_up(index)

    def sort_frame(frame, carry):
        value = measured[frame]
        total = jnp.zeros((256, 256), F32)
        for _ in range(3):
            piece = value.astype(BF16)
            value = value - piece.astype(F32)
            total = total + jnp.dot(piece, order_ref[...], preferred_element_type=F32)
        for block in range(2):
            turned[block] = total[:, block * 128:block * 128 + 128]
        for block in range(2):
            for parity in range(2):
                sorted_ref[frame, parity, :, block * 128:block * 128 + 128] = (
                    turned[block, pl.ds(parity, 128, stride=2), :])
        return carry

    load_frames.wait()
    share = measured.shape[0] // TOPS
    for index in range(TOPS):
        lax.fori_loop(index * share, (index + 1) * share, sort_frame, 0)
        halo.pass_on(index)
        halo.forward_corner(index)
    halo.finish()


def fetch(object_field, measured, order):
    dma = pltpu.SemaphoreType.DMA
    count = measured.shape[0]
    return pl.pallas_call(
        fetch_kernel,
        name="fetch",
        out_shape=(
            jax.ShapeDtypeStruct((2, 5, EXT, 128), F32),
            jax.ShapeDtypeStruct((count, 2, 128, 256), F32),
        ),
        in_specs=[HBM_SPEC, HBM_SPEC, VMEM_SPEC],
        out_specs=(VMEM_SPEC, VMEM_SPEC),
        scratch_shapes=[
            pltpu.VMEM((2, 256, 128), F32), pltpu.VMEM((count, 256, 256), F32), dma((7,)),
        ] + halo_sems(),
        compiler_params=pltpu.CompilerParams(
            collective_id=0, has_side_effects=True, vmem_limit_bytes=FETCH_VMEM),
    )(object_field, measured, order)


def halves(value):
    high = value.astype(BF16)
    low = (value - high.astype(F32)).astype(BF16)
    return high, low


def dot(left, right):
    return jnp.dot(left, right, preferred_element_type=F32)


def times_table(value, tables, index):
    high, low = halves(value)
    return dot(high, tables[index]) + dot(low, tables[index]) + dot(high, tables[index + 1])


def table_times(tables, index, value):
    high, low = halves(value)
    return dot(tables[index], high) + dot(tables[index + 1], high) + dot(tables[index], low)


def beside(a, b):
    return jnp.concatenate([a, b], axis=1)


def above(a, b):
    return jnp.concatenate([a, b], axis=0)


def frames_kernel(batch, counts_ref, first_ref, positions_ref, ext_ref, probe_ref, sorted_ref,
                  tables, grad_ref, probe_grad_ref):
    live = counts_ref[0, 0]
    first = jnp.minimum(first_ref[0, 0], live)
    start, end = (0, first) if batch == 0 else (first, live)
    for channel in range(2):
        for block in range(5):
            grad_ref[channel, block] = jnp.zeros((EXT, 128), F32)
    probe_grad_ref[...] = jnp.zeros_like(probe_grad_ref)
    lanes = lax.broadcasted_iota(jnp.int32, (256, 128), 1)

    def add_frame(frame, carry):
        row_start = positions_ref[0, frame]
        col_start = positions_ref[1, frame]
        block0 = col_start // 128
        shift = col_start - block0 * 128
        rows = pl.ds(row_start, 256)
        back_shift = jnp.bitwise_and(128 - shift, 127)

        window = []
        for channel in range(2):
            turned = [
                pltpu.roll(ext_ref[channel, block0 + block, rows, :], back_shift, 1)
                for block in range(3)
            ]
            keep = lanes < 128 - shift
            window.append([jnp.where(keep, turned[b], turned[b + 1]) for b in range(2)])
        probe = [[probe_ref[channel, :, b * 128:b * 128 + 128] for b in range(2)]
                 for channel in range(2)]
        exit_re = [probe[0][b] * window[0][b] - probe[1][b] * window[1][b] for b in range(2)]
        exit_im = [probe[0][b] * window[1][b] + probe[1][b] * window[0][b] for b in range(2)]
        y0 = times_table(beside(exit_re[0] + exit_re[1], exit_im[0] + exit_im[1]), tables, 0)
        y1 = times_table(beside(exit_re[0] - exit_re[1], exit_im[0] - exit_im[1]), tables, 2)

        def stacked(t0, t1):
            return above(beside(t0[:, :128], t1[:, :128]), beside(t0[:, 128:], t1[:, 128:]))

        w0 = table_times(tables, 4, stacked(y0[:128] + y0[128:], y1[:128] + y1[128:]))
        w1 = table_times(tables, 6, stacked(y0[:128] - y0[128:], y1[:128] - y1[128:]))

        def weighted(w, parity):
            re, im = w[:128], w[128:]
            residue = re * re + im * im - sorted_ref[frame, parity]
            return above(residue * re, residue * im)

        u0 = table_times(tables, 0, weighted(w0, 0))
        u1 = table_times(tables, 2, weighted(w1, 1))
        top, bottom = u0 + u1, u0 - u1
        z_re = above(top[:128], bottom[:128])
        z_im = above(top[128:], bottom[128:])
        v0 = times_table(beside(z_re[:, :128], z_im[:, :128]), tables, 4)
        v1 = times_table(beside(z_re[:, 128:], z_im[:, 128:]), tables, 6)
        back_re = [v0[:, :128] + v1[:, :128], v0[:, :128] - v1[:, :128]]
        back_im = [v0[:, 128:] + v1[:, 128:], v0[:, 128:] - v1[:, 128:]]

        for b in range(2):
            at = slice(b * 128, b * 128 + 128)
            probe_grad_ref[0, :, at] += window[0][b] * back_re[b] + window[1][b] * back_im[b]
            probe_grad_ref[1, :, at] += window[0][b] * back_im[b] - window[1][b] * back_re[b]
        before = lanes < shift
        zero = jnp.zeros((256, 128), F32)
        for channel in range(2):
            if channel == 0:
                term = [probe[0][b] * back_re[b] + probe[1][b] * back_im[b] for b in range(2)]
            else:
                term = [probe[0][b] * back_im[b] - probe[1][b] * back_re[b] for b in range(2)]
            turned = [pltpu.roll(term[b], shift, 1) for b in range(2)]
            adds = [
                jnp.where(before, zero, turned[0]),
                jnp.where(before, turned[0], turned[1]),
                jnp.where(before, turned[1], zero),
            ]
            for block in range(3):
                at = (channel, block0 + block, rows, slice(None))
                grad_ref[at] = grad_ref[at] + adds[block]
        return carry

    lax.fori_loop(start, end, add_frame, 0)


def frames(batch, counts, first, positions, ext, probe, ordered, tables):
    return pl.pallas_call(
        functools.partial(frames_kernel, batch),
        name=f"frames{batch}",
        out_shape=(
            jax.ShapeDtypeStruct((2, 5, EXT, 128), F32),
            jax.ShapeDtypeStruct((2, PROBE, PROBE), F32),
        ),
        in_specs=[SMEM_SPEC, SMEM_SPEC, SMEM_SPEC] + [VMEM_SPEC] * 4,
        out_specs=(VMEM_SPEC, VMEM_SPEC),
        compiler_params=pltpu.CompilerParams(vmem_limit_bytes=FRAMES_VMEM),
    )(counts, first, positions, ext, probe, ordered, tables)


AROUND = tuple((i, j) for i in range(4) for j in range(4) if i or j)


class Reduce:
    def __init__(self, grad, half, got_half, got_plane, got_z, sums, sems, row, col):
        self.grad, self.half, self.got_half = grad, half, got_half
        self.got_plane, self.got_z, self.sums, self.sems = got_plane, got_z, sums, sems
        self.row, self.col, self.core = row, col, row % 2
        self.y = (row % 8) // 2
        self.x = (row // 8) * 2 + col // 8
        self.z = col % 8

    def partner(self):
        return (self.row + 1 - 2 * self.core, self.col)

    def plane(self, i, j):
        x, y = (self.x + i) % 4, (self.y + j) % 4
        device = ((x // 2) * 8 + y * 2 + self.core, (x % 2) * 8 + self.z)
        return pl.ds(pl.multiple_of((x * 4 + y) * 16, 16), 16), device

    def over_z_to(self, step):
        z = (self.z + step) % 8
        return z, (self.row, (self.col // 8) * 8 + z)

    def peers(self):
        found = [self.partner()]
        found += [self.plane(i, j)[1] for i, j in AROUND]
        found += [self.over_z_to(step)[1] for step in range(1, 8)]
        return found

    def copy(self, src, dst, index, device):
        return remote(src, dst, self.sems.at[0, index], self.sems.at[1, index], device)

    def pair(self):
        return self.copy(self.grad.at[1 - self.core], self.got_half, 0, self.partner())

    def out(self, n):
        rows, device = self.plane(*AROUND[n])
        return self.copy(self.half.at[rows, :], self.got_plane.at[n], 1 + n, device)

    def along(self, step):
        return self.copy(
            self.got_z.at[self.z], self.got_z.at[self.z], 15 + step, self.over_z_to(step)[1])

    def back(self, n):
        rows = self.plane(0, 0)[0]
        mine = self.sums.at[self.core, rows, :]
        return self.copy(mine, mine, 23 + n, self.plane(*AROUND[n])[1])

    def back_pair(self):
        mine = self.sums.at[self.core]
        return self.copy(mine, mine, 38, self.partner())

    def begin(self):
        self.pair().start()

    def to_plane(self):
        self.pair().wait_recv()
        self.half[...] = self.grad[self.core] + self.got_half[...]
        for n in range(15):
            self.out(n).start()

    def to_z(self):
        for n in range(15):
            self.out(n).wait_recv()
        total = self.half[self.plane(0, 0)[0], :]
        for n in range(15):
            total = total + self.got_plane[n]
        self.got_z[self.z] = total
        for step in range(1, 8):
            self.along(step).start()

    def from_z(self):
        for step in range(1, 8):
            theirs = self.got_z.at[(self.z + 8 - step) % 8]
            self.copy(theirs, theirs, 15 + step, self.over_z_to(step)[1]).wait_recv()
        total = self.got_z[0]
        for z in range(1, 8):
            total = total + self.got_z[z]
        self.sums[self.core, self.plane(0, 0)[0], :] = total
        for n in range(15):
            self.back(n).start()

    def from_plane(self):
        for n in range(15):
            i, j = AROUND[n]
            theirs = self.sums.at[self.core, self.plane(4 - i, 4 - j)[0], :]
            self.copy(theirs, theirs, 23 + n, self.plane(i, j)[1]).wait_recv()
        self.back_pair().start()

    def end(self):
        theirs = self.sums.at[1 - self.core]
        self.copy(theirs, theirs, 38, self.partner()).wait_recv()

    def drain(self):
        self.pair().wait_send()
        for n in range(15):
            self.out(n).wait_send()
            self.back(n).wait_send()
        for step in range(1, 8):
            self.along(step).wait_send()
        self.back_pair().wait_send()


def exchange_kernel(refetch, object_ref, grad_ref, probe_ref, probe_grad_ref, out_ref, probe_out,
                    from_above, from_left, joined, half, got_half, got_plane, got_z, sums,
                    detour, down_sems, right_sems, reduce_sems, detour_sems, *sems):
    row, col = place()
    reduce = Reduce(
        probe_grad_ref, half, got_half, got_plane, got_z, sums, reduce_sems, row, col)
    barrier = pltpu.get_barrier_semaphore()
    greet_neighbours(barrier, row, col)
    greet_detour(barrier, row, col, DOWN_DETOUR)
    if refetch:
        greet_detour(barrier, row, col, UP_DETOUR)
    for device in reduce.peers():
        pl.semaphore_signal(barrier, inc=1, device_id=device, device_id_type=MESH)
    stops = [is_at(row, col, DOWN_DETOUR[hop]) for hop in range(3)]
    sends_down, takes_above = row < N_ROW - 1, row > 0
    sends_right, takes_left = col < N_COL - 1, col > 0
    if refetch:
        halo = Halo(out_ref, *sems, row, col)
        halo.clear_edges()

    @pl.when(row == 0)
    def _():
        for channel in range(2):
            for block in range(5):
                from_above[channel, block] = jnp.zeros((256, 128), F32)

    @pl.when(col == 0)
    def _():
        for channel in range(2):
            for block in range(2):
                from_left[channel, block] = jnp.zeros((TILE, 128), F32)

    greeted = 23 + neighbour_count(row, col) + detour_count(row, col, DOWN_DETOUR)
    if refetch:
        greeted = greeted + detour_count(row, col, UP_DETOUR)
    pl.semaphore_wait(barrier, greeted)

    def down(index, part):
        blocks = pl.ds(3, 2) if part == 0 else pl.ds(0, 3)
        start, rows = CHUNKS[index]
        return remote(
            grad_ref.at[:, blocks, pl.ds(384 + start, rows), :],
            from_above.at[:, blocks, pl.ds(start, rows), :],
            down_sems.at[0, part, index], down_sems.at[1, part, index],
            (jnp.minimum(row + 1, N_ROW - 1), col),
        )

    def detour_hop(hop, index):
        start, rows = CHUNKS[index]
        here = pl.ds(start, rows)
        source = detour.at[:, :, here, :] if hop else (
            grad_ref.at[:, pl.ds(0, 3), pl.ds(384 + start, rows), :])
        target = from_above.at[:, pl.ds(0, 3), here, :] if hop == 2 else detour.at[:, :, here, :]
        return remote(
            source, target, detour_sems.at[0, index],
            down_sems.at[1, 1, index] if hop == 2 else detour_sems.at[1, index],
            place_of(DOWN_DETOUR[hop + 1]),
        )

    def pass_on(index):
        for hop in (1, 2):
            @pl.when(stops[hop])
            def _(hop=hop):
                detour_hop(hop - 1, index).wait_recv()
                detour_hop(hop, index).start()

    sends_straight = sends_down & jnp.logical_not(stops[0])

    def send_corner(index):
        @pl.when(sends_down)
        def _():
            down(index, 0).start()

    def send_down(index):
        @pl.when(sends_straight)
        def _():
            down(index, 1).start()

        @pl.when(stops[0])
        def _():
            detour_hop(0, index).start()

    def right(index):
        start, rows = CHUNKS[index]
        if index in LOWS:
            source = grad_ref.at[:, pl.ds(3, 2), pl.ds(start, rows), :]
        else:
            source = joined.at[:, :, pl.ds(start, rows), :]
        return remote(
            source, from_left.at[:, :, pl.ds(start, rows), :],
            right_sems.at[0, index], right_sems.at[1, index],
            (row, jnp.minimum(col + 1, N_COL - 1)),
        )

    def send_right(index):
        @pl.when(sends_right)
        def _():
            right(index).start()

    def join(index):
        start, rows = CHUNKS[index]
        at = slice(start, start + rows)

        @pl.when(takes_above)
        def _():
            down(index, 0).wait_recv()

        for channel in range(2):
            for block in range(2):
                joined[channel, block, at] = (
                    grad_ref[channel, 3 + block, at] + from_above[channel, 3 + block, at])
        send_right(index)

    def update(index):
        start, rows = CHUNKS[index]
        at = slice(start, start + rows)
        if index < TOPS:
            @pl.when(takes_above)
            def _():
                down(index, 1).wait_recv()

        @pl.when(takes_left)
        def _():
            right(index).wait_recv()

        for channel in range(2):
            for block in range(3):
                grad = grad_ref[channel, block, at]
                if index < TOPS:
                    grad = grad + from_above[channel, block, at]
                if block < 2:
                    grad = grad + from_left[channel, block, at]
                value = object_ref[channel, block, at] - 0.1 * grad
                if refetch:
                    out_ref[channel, block, at] = value
                else:
                    out_ref[channel, at, block * 128:block * 128 + 128] = value
        if refetch:
            halo.send_left(index)
            if index < TOPS:
                halo.send_up(index)

    def forward(index):
        if refetch:
            halo.forward_corner(index)

    def pass_up(index):
        if refetch:
            halo.pass_on(index)

    reduce.begin()
    send_right(4)
    send_corner(0)
    send_corner(1)
    reduce.to_plane()
    send_corner(2)
    send_corner(3)
    for index in range(TOPS):
        send_down(index)
    join(0)
    join(1)
    pass_on(0)
    update(4)
    pass_on(1)
    reduce.to_z()
    join(2)
    join(3)
    send_right(5)
    pass_on(2)
    update(0)
    pass_on(3)
    update(1)
    reduce.from_z()
    forward(0)
    update(2)
    forward(1)
    update(3)
    update(5)
    pass_up(0)
    pass_up(1)
    reduce.from_plane()
    for index in (2, 3):
        forward(index)
        pass_up(index)
    reduce.end()
    step_size = 0.5 / math.sqrt(N_ROW * N_COL * 8)
    probe_out[...] = probe_ref[...] - step_size * sums[...]
    if refetch:
        halo.finish()
    reduce.drain()

    @pl.when(sends_down)
    def _():
        for index in range(TOPS):
            down(index, 0).wait_send()

    @pl.when(sends_straight)
    def _():
        for index in range(TOPS):
            down(index, 1).wait_send()

    for hop in range(3):
        @pl.when(stops[hop])
        def _(hop=hop):
            for index in range(TOPS):
                detour_hop(hop, index).wait_send()

    @pl.when(sends_right)
    def _():
        for index in range(EVERY):
            right(index).wait_send()


def exchange(refetch, ext, grad, probe, probe_grad):
    dma = pltpu.SemaphoreType.DMA
    out = (2, 5, EXT, 128) if refetch else (2, TILE, TILE)
    return pl.pallas_call(
        functools.partial(exchange_kernel, refetch),
        name=f"exchange{int(refetch)}",
        out_shape=(
            jax.ShapeDtypeStruct(out, F32), jax.ShapeDtypeStruct((2, PROBE, PROBE), F32)),
        in_specs=[VMEM_SPEC] * 4,
        out_specs=(VMEM_SPEC, VMEM_SPEC),
        scratch_shapes=[
            pltpu.VMEM((2, 5, 256, 128), F32),
            pltpu.VMEM((2, 2, TILE, 128), F32),
            pltpu.VMEM((2, 2, 256, 128), F32),
            pltpu.VMEM((256, 256), F32),
            pltpu.VMEM((256, 256), F32),
            pltpu.VMEM((15, 16, 256), F32),
            pltpu.VMEM((8, 16, 256), F32),
            pltpu.VMEM((2, 256, 256), F32),
            pltpu.VMEM((2, 3, 256, 128), F32),
            dma((2, 2, TOPS)),
            dma((2, EVERY)),
            dma((2, 39)),
            dma((2, TOPS)),
        ] + (halo_sems() if refetch else []),
        compiler_params=pltpu.CompilerParams(
            collective_id=1 + int(refetch), has_side_effects=True,
            vmem_limit_bytes=EXCHANGE_VMEM),
    )(ext, grad, probe, probe_grad)


def per_device(object_field, illumination, measured, positions, frame_counts, first_count):
    tables = jnp.asarray(dft_tables())
    order = jnp.asarray(deinterleave_table())
    positions = positions[0, 0].T
    probe = illumination
    ext, ordered = fetch(object_field, measured[0, 0], order)
    grad, probe_grad = frames(
        0, frame_counts, first_count, positions, ext, probe, ordered, tables)
    ext, probe = exchange(True, ext, grad, probe, probe_grad)
    grad, probe_grad = frames(
        1, frame_counts, first_count, positions, ext, probe, ordered, tables)
    new_object, probe = exchange(False, ext, grad, probe, probe_grad)
    return new_object, probe


def solution(mesh):
    in_specs = (
        P(None, "row", "col"),
        P(),
        P("row", "col", None, None, None),
        P("row", "col", None, None),
        P("row", "col"),
        P("row", "col"),
    )
    out_specs = (P(None, "row", "col"), P())
    return jax.shard_map(
        per_device, mesh=mesh, in_specs=in_specs, out_specs=out_specs, check_vma=False
    )
```

time: 187 us -> 150 us (0.80); the launches traced: 188 us -> 149 us
  Pallas kernels: 180 us -> 141 us
    pallas_call x2, Pallas kernels: 138 us -> 101 us  [exchange(): pl.pallas_call(functools.partial(exchange_kernel, refetch), name=f'exchan...]
    pallas_call x1, Pallas kernels: 27.5 us -> 22.6 us  [fetch(): pl.pallas_call(fetch_kernel, name='fetch', out_shape=(jax.ShapeDtypeStruc...]
    unnamed x3 -> x14, local copies, waits for them, and re-layouts: 2.37 us -> 5.58 us
    pallas_call x2, Pallas kernels: 14 us -> 16.9 us  [frames(): pl.pallas_call(functools.partial(frames_kernel, batch), name=f'frames{bat...]
    reshape x2 -> x0, local copies, waits for them, and re-layouts: 2.7 us -> none  [the longest x1 1.87 us: from_blocks(): blocks.reshape(2, 2, 256, 128).transpose(0, 2, 1, 3).reshape(2, 256, 256)]
where the time goes in v1:
time: 150 us; the launch traced here: 149 us
  Pallas kernels  141 us (94%)
  local copies, waits for them, and re-layouts  5.58 us (4%)
  between operations  2.09 us (1%)
    pallas_call x2, Pallas kernels, exchange(): pl.pallas_call(functools.partial(exchange_kernel, refetch), name=f'exchan...  101 us
    pallas_call x1, Pallas kernels, fetch(): pl.pallas_call(fetch_kernel, name='fetch', out_shape=(jax.ShapeDtypeStruc...  22.6 us
    pallas_call x2, Pallas kernels, frames(): pl.pallas_call(functools.partial(frames_kernel, batch), name=f'frames{bat...  16.9 us
    unnamed x14, local copies, waits for them, and re-layouts  5.58 us

profile of v1, /device:TPU:1, one launch (start us, length us, event | category | flops | bytes accessed | tf_op | source)
XLA Modules:
  0.0 148.6 jit_solution(10707252801858774988)
XLA Ops:
  0.6 0.0 copy-start
  2.0 0.0 copy-start.1
  2.0 1.6 %copy-done.1 = f32[1,1,8,256,256]{4,3,2,1,0:T(8,128)S(1)} copy-done((f32[1,1,8,256,256]{4,3,2,1,0:T(8,128)S(1)}, f32[1,1,8,256,256]{4,3,2,1,0:T(8,128)}, u32[]{:S(2)}) %copy-start.1) | copy-done | bytes 2097176
  3.6 0.0 copy-start.3
  3.6 1.3 copy-done.3
  4.9 0.0 copy-start.4
  4.9 0.9 copy-done.4
  5.8 0.0 copy-start.2
  5.8 0.0 copy-start.5
  5.8 22.6 %fetch.1 = (f32[2,5,640,128]{3,2,1,0:T(8,128)S(1)}, f32[8,2,128,256]{3,2,1,0:T(8,128)S(1)}) custom-call(f32[2,384,384]{2,1,0:T(8,128)S(1)} %copy-done.3, f32[8,256,256]{2,1,0:T(8,128)S(1)} %bitcast.4, bf16[256,256]{1,0:T(8,128)(2,1)S(1)} %copy-done.4), custom_call_target="tpu_custom_call" | custom-call | tf_op jit(solution)/shard_map/fetch/pallas_call | solution.py:305
  28.4 0.0 copy-done
  28.4 0.0 copy-done.2
  28.4 0.0 copy-done.5
  28.5 0.8 frames0.1
  29.3 63.5 %exchange1.1 = (f32[2,5,640,128]{3,2,1,0:T(8,128)S(1)}, f32[2,256,256]{2,1,0:T(8,128)S(1)}) custom-call(f32[2,5,640,128]{3,2,1,0:T(8,128)S(1)} %get-tuple-element.10.ext_ref.object_ref, f32[2,5,640,128]{3,2,1,0:T(8,128)S(1)} %get-tuple-element.12.grad_ref, f32[2,256,256]{2,1,0:T(8,128)S(1)} %copy-done.2, f32[2,256,256]{2,1,0:T(8,128)S(1)} %get-tuple-element.13.probe_grad_ref), custom_call_target="tpu_custom_call" | custom-call | tf_op jit(solution)/shard_map/exchange1/pallas_call | solution.py:764
  92.7 16.1 %frames1.1 = (f32[2,5,640,128]{3,2,1,0:T(8,128)S(1)}, f32[2,256,256]{2,1,0:T(8,128)S(1)}) custom-call(s32[1,1]{1,0:T(1,128)S(6)} %copy.12.counts_ref, s32[1,1]{1,0:T(1,128)S(6)} %copy.13.first_ref, s32[2,8]{1,0:T(2,128)S(1)} %bitcast.6, f32[2,5,640,128]{3,2,1,0:T(8,128)S(1)} %get-tuple-element.14.ext_ref.object_ref, ...), custom_call_target="tpu_custom_call" | custom-call | tf_op jit(solution)/shard_map/frames1/pallas_call | solution.py:431
  108.8 38.0 %exchange0.1 = (f32[2,384,384]{2,1,0:T(8,128)S(1)}, f32[2,256,256]{2,1,0:T(8,128)S(1)}) custom-call(f32[2,5,640,128]{3,2,1,0:T(8,128)S(1)} %get-tuple-element.14.ext_ref.object_ref, f32[2,5,640,128]{3,2,1,0:T(8,128)S(1)} %get-tuple-element.16.grad_ref, f32[2,256,256]{2,1,0:T(8,128)S(1)} %get-tuple-element.15.probe_ref, ...), custom_call_target="tpu_custom_call" | custom-call | tf_op jit(solution)/shard_map/exchange0/pallas_call | solution.py:764
  146.8 1.0 copy.14
  147.8 0.8 copy.15
Async XLA Ops:
  0.6 27.8 %copy-start = (bf16[8,256,256]{2,1,0:T(8,128)(2,1)S(1)}, bf16[8,256,256]{2,1,0:T(8,128)(2,1)}, u32[]{:S(2)}) copy-start(bf16[8,256,256]{2,1,0:T(8,128)(2,1)} %constant.4.clone.tables) | copy-start | bytes 3145732
  2.0 1.6 %copy-start.1 = (f32[1,1,8,256,256]{4,3,2,1,0:T(8,128)S(1)}, f32[1,1,8,256,256]{4,3,2,1,0:T(8,128)}, u32[]{:S(2)}) copy-start(f32[1,1,8,256,256]{4,3,2,1,0:T(8,128)} %param.10) | copy-start | bytes 6291460
  3.6 1.3 copy-start.3
  4.9 0.9 copy-start.4
  5.8 22.6 %copy-start.2 = (f32[2,256,256]{2,1,0:T(8,128)S(1)}, f32[2,256,256]{2,1,0:T(8,128)}, u32[]{:S(2)}) copy-start(f32[2,256,256]{2,1,0:T(8,128)} %probe_ref.3) | copy-start | bytes 1572868
  5.8 22.7 %copy-start.5 = (s32[1,1,8,2]{2,3,1,0:T(2,128)S(1)}, s32[1,1,8,2]{2,3,1,0:T(2,128)}, u32[]{:S(2)}) copy-start(s32[1,1,8,2]{2,3,1,0:T(2,128)} %param.11) | copy-start | bytes 196

commit v2 on v1

--- a/solution.py
+++ b/solution.py
@@ -61,8 +61,8 @@
     )
 
 
-UP_DETOUR = ((8, 15), (14, 15), (6, 7), (7, 15))
-DOWN_DETOUR = ((7, 0), (1, 0), (9, 8), (8, 0))
+UP_DETOURS = (((8, 15), (14, 15), (6, 7), (7, 15)),)
+DOWN_DETOURS = (((7, 0), (1, 0), (9, 8), (8, 0)), ((7, 15), (1, 15), (9, 7), (8, 15)))
 
 
 def is_at(row, col, device):
@@ -73,20 +73,36 @@
     return jnp.int32(device[0]), jnp.int32(device[1])
 
 
-def greet_detour(barrier, row, col, detour):
-    for hop in range(3):
-        for here, there in ((detour[hop], detour[hop + 1]), (detour[hop + 1], detour[hop])):
-            @pl.when(is_at(row, col, here))
-            def _(there=there):
-                pl.semaphore_signal(
-                    barrier, inc=1, device_id=place_of(there), device_id_type=MESH)
-
-
-def detour_count(row, col, detour):
-    one, two, none = jnp.int32(1), jnp.int32(2), jnp.int32(0)
-    ends = is_at(row, col, detour[0]) | is_at(row, col, detour[3])
-    middles = is_at(row, col, detour[1]) | is_at(row, col, detour[2])
-    return jnp.where(ends, one, none) + jnp.where(middles, two, none)
+class Detour:
+    def __init__(self, paths, row, col):
+        self.paths, self.row, self.col = paths, row, col
+        self.first = [is_at(row, col, paths[0][stop]) for stop in range(4)]
+        self.stops = [
+            functools.reduce(jnp.logical_or, [is_at(row, col, path[stop]) for path in paths])
+            for stop in range(4)
+        ]
+
+    def next_place(self, hop):
+        row, col = place_of(self.paths[0][hop + 1])
+        for path in self.paths[1:]:
+            other_row, other_col = place_of(path[hop + 1])
+            here = is_at(self.row, self.col, path[hop])
+            row, col = jnp.where(here, other_row, row), jnp.where(here, other_col, col)
+        return row, col
+
+    def greet(self, barrier):
+        for path in self.paths:
+            for hop in range(3):
+                for here, there in ((path[hop], path[hop + 1]), (path[hop + 1], path[hop])):
+                    @pl.when(is_at(self.row, self.col, here))
+                    def _(there=there):
+                        pl.semaphore_signal(
+                            barrier, inc=1, device_id=place_of(there), device_id_type=MESH)
+
+    def count(self):
+        one, two, none = jnp.int32(1), jnp.int32(2), jnp.int32(0)
+        return jnp.where(self.stops[0] | self.stops[3], one, none) + jnp.where(
+            self.stops[1] | self.stops[2], two, none)
 
 
 def greet_neighbours(barrier, row, col):
@@ -114,11 +130,11 @@
 
 
 class Halo:
-    def __init__(self, ext, detour, left_sems, up_sems, corner_sems, detour_sems, row, col):
+    def __init__(self, ext, way, detour, left_sems, up_sems, corner_sems, detour_sems, row, col):
         self.ext, self.row, self.col = ext, row, col
         self.left_sems, self.up_sems, self.corner_sems = left_sems, up_sems, corner_sems
         self.detour, self.detour_sems = detour, detour_sems
-        self.stops = [is_at(row, col, UP_DETOUR[hop]) for hop in range(3)]
+        self.way, self.stops = way, way.stops
         self.sends_left, self.takes_right = col > 0, col < N_COL - 1
         self.sends_up, self.takes_below = row > 0, row < N_ROW - 1
         self.sends_direct = self.sends_up & jnp.logical_not(self.stops[0])
@@ -157,7 +173,7 @@
             source.at[:, pl.ds(0, 3), pl.ds(start, rows), :], target,
             self.detour_sems.at[0, index],
             self.up_sems.at[1, index] if last else self.detour_sems.at[1, index],
-            place_of(UP_DETOUR[hop + 1]),
+            self.way.next_place(hop),
         )
 
     def pass_on(self, index):
@@ -252,7 +268,8 @@
     row, col = place()
     barrier = pltpu.get_barrier_semaphore()
     greet_neighbours(barrier, row, col)
-    greet_detour(barrier, row, col, UP_DETOUR)
+    way = Detour(UP_DETOURS, row, col)
+    way.greet(barrier)
     loads = []
     for channel in range(2):
         for block in range(3):
@@ -265,11 +282,11 @@
             loads.append(load)
     load_frames = pltpu.make_async_copy(measured_ref, measured, load_sems.at[6])
     load_frames.start()
-    halo = Halo(ext_ref, *sems, row, col)
+    halo = Halo(ext_ref, way, *sems, row, col)
     halo.clear_edges()
     for load in loads:
         load.wait()
-    pl.semaphore_wait(barrier, neighbour_count(row, col) + detour_count(row, col, UP_DETOUR))
+    pl.semaphore_wait(barrier, neighbour_count(row, col) + way.count())
     for index in range(EVERY):
         halo.send_left(index)
     for index in range(TOPS):
@@ -316,7 +333,7 @@
         ] + halo_sems(),
         compiler_params=pltpu.CompilerParams(
             collective_id=0, has_side_effects=True, vmem_limit_bytes=FETCH_VMEM),
-    )(object_field, measured, order)
+    )(*(pltpu.with_memory_space_constraint(a, pltpu.HBM) for a in (object_field, measured)), order)
 
 
 def halves(value):
@@ -553,22 +570,30 @@
         probe_grad_ref, half, got_half, got_plane, got_z, sums, reduce_sems, row, col)
     barrier = pltpu.get_barrier_semaphore()
     greet_neighbours(barrier, row, col)
-    greet_detour(barrier, row, col, DOWN_DETOUR)
+    down_way = Detour(DOWN_DETOURS if refetch else DOWN_DETOURS[:1], row, col)
+    down_way.greet(barrier)
     if refetch:
-        greet_detour(barrier, row, col, UP_DETOUR)
+        up_way = Detour(UP_DETOURS, row, col)
+        up_way.greet(barrier)
     for device in reduce.peers():
         pl.semaphore_signal(barrier, inc=1, device_id=device, device_id_type=MESH)
-    stops = [is_at(row, col, DOWN_DETOUR[hop]) for hop in range(3)]
+    stops = (down_way.first, down_way.stops)
     sends_down, takes_above = row < N_ROW - 1, row > 0
     sends_right, takes_left = col < N_COL - 1, col > 0
     if refetch:
-        halo = Halo(out_ref, *sems, row, col)
+        halo = Halo(out_ref, up_way, *sems, row, col)
         halo.clear_edges()
+
+    @pl.when((row == 0) | (col == N_COL - 1))
+    def _():
+        for channel in range(2):
+            for block in (3, 4):
+                from_above[channel, block] = jnp.zeros((256, 128), F32)
 
     @pl.when(row == 0)
     def _():
         for channel in range(2):
-            for block in range(5):
+            for block in range(3):
                 from_above[channel, block] = jnp.zeros((256, 128), F32)
 
     @pl.when(col == 0)
@@ -577,9 +602,9 @@
             for block in range(2):
                 from_left[channel, block] = jnp.zeros((TILE, 128), F32)
 
-    greeted = 23 + neighbour_count(row, col) + detour_count(row, col, DOWN_DETOUR)
+    greeted = 23 + neighbour_count(row, col) + down_way.count()
     if refetch:
-        greeted = greeted + detour_count(row, col, UP_DETOUR)
+        greeted = greeted + up_way.count()
     pl.semaphore_wait(barrier, greeted)
 
     def down(index, part):
@@ -592,40 +617,38 @@
             (jnp.minimum(row + 1, N_ROW - 1), col),
         )
 
-    def detour_hop(hop, index):
+    def detour_hop(hop, index, part):
         start, rows = CHUNKS[index]
+        blocks = pl.ds(3, 2) if part == 0 else pl.ds(0, 3)
         here = pl.ds(start, rows)
-        source = detour.at[:, :, here, :] if hop else (
-            grad_ref.at[:, pl.ds(0, 3), pl.ds(384 + start, rows), :])
-        target = from_above.at[:, pl.ds(0, 3), here, :] if hop == 2 else detour.at[:, :, here, :]
+        source = detour.at[:, blocks, here, :] if hop else (
+            grad_ref.at[:, blocks, pl.ds(384 + start, rows), :])
+        target = (from_above if hop == 2 else detour).at[:, blocks, here, :]
         return remote(
-            source, target, detour_sems.at[0, index],
-            down_sems.at[1, 1, index] if hop == 2 else detour_sems.at[1, index],
-            place_of(DOWN_DETOUR[hop + 1]),
+            source, target, detour_sems.at[0, part, index],
+            (down_sems if hop == 2 else detour_sems).at[1, part, index],
+            down_way.next_place(hop),
         )
 
-    def pass_on(index):
+    def pass_on(index, part):
         for hop in (1, 2):
-            @pl.when(stops[hop])
+            @pl.when(stops[part][hop])
             def _(hop=hop):
-                detour_hop(hop - 1, index).wait_recv()
-                detour_hop(hop, index).start()
-
-    sends_straight = sends_down & jnp.logical_not(stops[0])
-
-    def send_corner(index):
-        @pl.when(sends_down)
-        def _():
-            down(index, 0).start()
-
-    def send_down(index):
-        @pl.when(sends_straight)
-        def _():
-            down(index, 1).start()
-
-        @pl.when(stops[0])
-        def _():
-            detour_hop(0, index).start()
+                detour_hop(hop - 1, index, part).wait_recv()
+                detour_hop(hop, index, part).start()
+
+    needs = (sends_down & sends_right, sends_down)
+    takes = (takes_above & sends_right, takes_above)
+    straight = [needs[part] & jnp.logical_not(stops[part][0]) for part in range(2)]
+
+    def send_down(index, part):
+        @pl.when(straight[part])
+        def _():
+            down(index, part).start()
+
+        @pl.when(stops[part][0])
+        def _():
+            detour_hop(0, index, part).start()
 
     def right(index):
         start, rows = CHUNKS[index]
@@ -648,7 +671,7 @@
         start, rows = CHUNKS[index]
         at = slice(start, start + rows)
 
-        @pl.when(takes_above)
+        @pl.when(takes[0])
         def _():
             down(index, 0).wait_recv()
 
@@ -697,60 +720,70 @@
 
     reduce.begin()
     send_right(4)
-    send_corner(0)
-    send_corner(1)
+    send_right(5)
+    send_down(0, 0)
+    send_down(1, 0)
     reduce.to_plane()
-    send_corner(2)
-    send_corner(3)
+    send_down(2, 0)
+    send_down(3, 0)
     for index in range(TOPS):
-        send_down(index)
+        send_down(index, 1)
+    pass_on(0, 0)
+    pass_on(1, 0)
+    update(4)
+    reduce.to_z()
     join(0)
     join(1)
-    pass_on(0)
-    update(4)
-    pass_on(1)
-    reduce.to_z()
+    pass_on(2, 0)
+    pass_on(3, 0)
     join(2)
     join(3)
-    send_right(5)
-    pass_on(2)
-    update(0)
-    pass_on(3)
-    update(1)
-    reduce.from_z()
-    forward(0)
-    update(2)
-    forward(1)
-    update(3)
-    update(5)
-    pass_up(0)
-    pass_up(1)
-    reduce.from_plane()
-    for index in (2, 3):
-        forward(index)
-        pass_up(index)
+    pass_on(0, 1)
+    pass_on(1, 1)
+    if refetch:
+        update(0)
+        reduce.from_z()
+        update(1)
+        pass_on(2, 1)
+        pass_on(3, 1)
+        forward(0)
+        update(2)
+        pass_up(0)
+        forward(1)
+        update(3)
+        update(5)
+        pass_up(1)
+        reduce.from_plane()
+        for index in (2, 3):
+            forward(index)
+            pass_up(index)
+    else:
+        update(5)
+        reduce.from_z()
+        pass_on(2, 1)
+        pass_on(3, 1)
+        update(0)
+        update(1)
+        reduce.from_plane()
+        update(2)
+        update(3)
     reduce.end()
     step_size = 0.5 / math.sqrt(N_ROW * N_COL * 8)
     probe_out[...] = probe_ref[...] - step_size * sums[...]
     if refetch:
         halo.finish()
     reduce.drain()
-
-    @pl.when(sends_down)
-    def _():
-        for index in range(TOPS):
-            down(index, 0).wait_send()
-
-    @pl.when(sends_straight)
-    def _():
-        for index in range(TOPS):
-            down(index, 1).wait_send()
-
-    for hop in range(3):
-        @pl.when(stops[hop])
-        def _(hop=hop):
+    for part in range(2):
+        @pl.when(straight[part])
+        def _(part=part):
             for index in range(TOPS):
-                detour_hop(hop, index).wait_send()
+                down(index, part).wait_send()
+
+        for hop in range(3):
+            @pl.when(stops[part][hop])
+            def _(hop=hop, part=part):
+                for index in range(TOPS):
+                    detour_hop(hop, index, part).wait_send()
 
     @pl.when(sends_right)
     def _():
@@ -777,11 +810,11 @@
             pltpu.VMEM((15, 16, 256), F32),
             pltpu.VMEM((8, 16, 256), F32),
             pltpu.VMEM((2, 256, 256), F32),
-            pltpu.VMEM((2, 3, 256, 128), F32),
+            pltpu.VMEM((2, 5, 256, 128), F32),
             dma((2, 2, TOPS)),
             dma((2, EVERY)),
             dma((2, 39)),
-            dma((2, TOPS)),
+            dma((2, 2, TOPS)),
         ] + (halo_sems() if refetch else []),
         compiler_params=pltpu.CompilerParams(
             collective_id=1 + int(refetch), has_side_effects=True,

time: 150 us -> 140 us (0.933)
  Pallas kernels: 141 us -> 135 us
  local copies, waits for them, and re-layouts: 5.58 us -> 2.72 us
    pallas_call x2, Pallas kernels: 16.9 us -> 7.31 us  [frames(): pl.pallas_call(functools.partial(frames_kernel, batch), name=f'frames{bat...]
    pallas_call x2, Pallas kernels: 101 us -> 105 us  [exchange(): pl.pallas_call(functools.partial(exchange_kernel, refetch), name=f'exchan...]
    unnamed x14 -> x10, local copies, waits for them, and re-layouts: 5.58 us -> 2.72 us
where the time goes in v2:
time: 140 us
  Pallas kernels  135 us (96%)
  local copies, waits for them, and re-layouts  2.72 us (2%)
  between operations  2.13 us (2%)
    pallas_call x2, Pallas kernels, exchange(): pl.pallas_call(functools.partial(exchange_kernel, refetch), name=f'exchan...  105 us
    pallas_call x1, Pallas kernels, fetch(): pl.pallas_call(fetch_kernel, name='fetch', out_shape=(jax.ShapeDtypeStruc...  22.6 us
    pallas_call x2, Pallas kernels, frames(): pl.pallas_call(functools.partial(frames_kernel, batch), name=f'frames{bat...  7.31 us

profile of v2, /device:TPU:1, one launch (start us, length us, event | category | flops | bytes accessed | tf_op | source)
XLA Modules:
  0.0 140.0 jit_solution(16421714966469966319)
XLA Ops:
  0.6 0.0 copy-start
  0.6 0.0 copy-start.1
  2.1 0.0 copy-start.2
  2.1 0.9 copy-done.2
  3.0 0.0 copy-start.3
  3.0 22.6 %fetch.1 = (f32[2,5,640,128]{3,2,1,0:T(8,128)S(1)}, f32[8,2,128,256]{3,2,1,0:T(8,128)S(1)}) custom-call(f32[2,384,384]{2,1,0:T(8,128)} %object_ref.1, f32[8,256,256]{2,1,0:T(8,128)} %bitcast.6, bf16[256,256]{1,0:T(8,128)(2,1)S(1)} %copy-done.2), custom_call_target="tpu_custom_call" | custom-call | tf_op jit(solution)/shard_map/fetch/pallas_call | solution.py:322
  25.6 0.0 copy-done
  25.6 0.0 copy-done.1
  25.6 0.0 copy-done.3
  25.6 2.7 %frames0.1 = (f32[2,5,640,128]{3,2,1,0:T(8,128)S(1)}, f32[2,256,256]{2,1,0:T(8,128)S(1)}) custom-call(s32[1,1]{1,0:T(1,128)S(6)} %copy.12.counts_ref, s32[1,1]{1,0:T(1,128)S(6)} %copy.13.first_ref, s32[2,8]{1,0:T(2,128)S(1)} %bitcast.4, f32[2,5,640,128]{3,2,1,0:T(8,128)S(1)} %get-tuple-element.10.ext_ref.object_ref, f32[2,256,256]{2,1,0:T(8,128)S(1)} %copy-done.1, ...), custom_call_target="tpu_custom_call" | custom-call | tf_op jit(solution)/shard_map/frames0/pallas_call | solution.py:448
  28.3 57.9 %exchange1.1 = (f32[2,5,640,128]{3,2,1,0:T(8,128)S(1)}, f32[2,256,256]{2,1,0:T(8,128)S(1)}) custom-call(f32[2,5,640,128]{3,2,1,0:T(8,128)S(1)} %get-tuple-element.10.ext_ref.object_ref, f32[2,5,640,128]{3,2,1,0:T(8,128)S(1)} %get-tuple-element.12.grad_ref, f32[2,256,256]{2,1,0:T(8,128)S(1)} %copy-done.1, f32[2,256,256]{2,1,0:T(8,128)S(1)} %get-tuple-element.13.probe_grad_ref), custom_call_target="tpu_custom_call" | custom-call | tf_op jit(solution)/shard_map/exchange1/pallas_call | solution.py:797
  86.2 4.6 %frames1.1 = (f32[2,5,640,128]{3,2,1,0:T(8,128)S(1)}, f32[2,256,256]{2,1,0:T(8,128)S(1)}) custom-call(s32[1,1]{1,0:T(1,128)S(6)} %copy.12.counts_ref, s32[1,1]{1,0:T(1,128)S(6)} %copy.13.first_ref, s32[2,8]{1,0:T(2,128)S(1)} %bitcast.5, f32[2,5,640,128]{3,2,1,0:T(8,128)S(1)} %get-tuple-element.14.ext_ref.object_ref, ...), custom_call_target="tpu_custom_call" | custom-call | tf_op jit(solution)/shard_map/frames1/pallas_call | solution.py:448
  90.8 47.3 %exchange0.1 = (f32[2,384,384]{2,1,0:T(8,128)S(1)}, f32[2,256,256]{2,1,0:T(8,128)S(1)}) custom-call(f32[2,5,640,128]{3,2,1,0:T(8,128)S(1)} %get-tuple-element.14.ext_ref.object_ref, f32[2,5,640,128]{3,2,1,0:T(8,128)S(1)} %get-tuple-element.16.grad_ref, f32[2,256,256]{2,1,0:T(8,128)S(1)} %get-tuple-element.15.probe_ref, ...), custom_call_target="tpu_custom_call" | custom-call | tf_op jit(solution)/shard_map/exchange0/pallas_call | solution.py:797
  138.2 1.0 copy.14
  139.2 0.8 copy.15
Async XLA Ops:
  0.6 25.0 %copy-start = (bf16[8,256,256]{2,1,0:T(8,128)(2,1)S(1)}, bf16[8,256,256]{2,1,0:T(8,128)(2,1)}, u32[]{:S(2)}) copy-start(bf16[8,256,256]{2,1,0:T(8,128)(2,1)} %constant.4.clone.tables) | copy-start | bytes 3145732
  0.6 25.0 %copy-start.1 = (f32[2,256,256]{2,1,0:T(8,128)S(1)}, f32[2,256,256]{2,1,0:T(8,128)}, u32[]{:S(2)}) copy-start(f32[2,256,256]{2,1,0:T(8,128)} %probe_ref.3) | copy-start | bytes 1572868
  2.1 0.9 copy-start.2
  3.0 22.7 %copy-start.3 = (s32[1,1,8,2]{2,3,1,0:T(2,128)S(1)}, s32[1,1,8,2]{2,3,1,0:T(2,128)}, u32[]{:S(2)}) copy-start(s32[1,1,8,2]{2,3,1,0:T(2,128)} %param.11) | copy-start | bytes 196

commit v3 on v2

--- a/solution.py
+++ b/solution.py
@@ -375,54 +375,73 @@
     probe_grad_ref[...] = jnp.zeros_like(probe_grad_ref)
     lanes = lax.broadcasted_iota(jnp.int32, (256, 128), 1)
 
-    def add_frame(frame, carry):
-        row_start = positions_ref[0, frame]
-        col_start = positions_ref[1, frame]
+    def load_window(frame):
+        row_start, col_start = positions_ref[0, frame], positions_ref[1, frame]
         block0 = col_start // 128
         shift = col_start - block0 * 128
         rows = pl.ds(row_start, 256)
         back_shift = jnp.bitwise_and(128 - shift, 127)
-
+        keep = lanes < 128 - shift
         window = []
         for channel in range(2):
             turned = [
                 pltpu.roll(ext_ref[channel, block0 + block, rows, :], back_shift, 1)
                 for block in range(3)
             ]
-            keep = lanes < 128 - shift
             window.append([jnp.where(keep, turned[b], turned[b + 1]) for b in range(2)])
-        probe = [[probe_ref[channel, :, b * 128:b * 128 + 128] for b in range(2)]
-                 for channel in range(2)]
-        exit_re = [probe[0][b] * window[0][b] - probe[1][b] * window[1][b] for b in range(2)]
-        exit_im = [probe[0][b] * window[1][b] + probe[1][b] * window[0][b] for b in range(2)]
-        y0 = times_table(beside(exit_re[0] + exit_re[1], exit_im[0] + exit_im[1]), tables, 0)
-        y1 = times_table(beside(exit_re[0] - exit_re[1], exit_im[0] - exit_im[1]), tables, 2)
-
-        def stacked(t0, t1):
-            return above(beside(t0[:, :128], t1[:, :128]), beside(t0[:, 128:], t1[:, 128:]))
-
-        w0 = table_times(tables, 4, stacked(y0[:128] + y0[128:], y1[:128] + y1[128:]))
-        w1 = table_times(tables, 6, stacked(y0[:128] - y0[128:], y1[:128] - y1[128:]))
-
-        def weighted(w, parity):
-            re, im = w[:128], w[128:]
+        return window, block0, shift, rows
+
+    def load_probe():
+        return [[probe_ref[channel, :, b * 128:b * 128 + 128] for b in range(2)]
+                for channel in range(2)]
+
+    def stacked(t0, t1):
+        return above(beside(t0[:, :128], t1[:, :128]), beside(t0[:, 128:], t1[:, 128:]))
+
+    def across(window):
+        probe = load_probe()
+        re = [probe[0][b] * window[0][b] - probe[1][b] * window[1][b] for b in range(2)]
+        im = [probe[0][b] * window[1][b] + probe[1][b] * window[0][b] for b in range(2)]
+        return (times_table(beside(re[0] + re[1], im[0] + im[1]), tables, 0),
+                times_table(beside(re[0] - re[1], im[0] - im[1]), tables, 2))
+
+    def along(y):
+        y0, y1 = y
+        return (table_times(tables, 4, stacked(y0[:128] + y0[128:], y1[:128] + y1[128:])),
+                table_times(tables, 6, stacked(y0[:128] - y0[128:], y1[:128] - y1[128:])))
+
+    def along_back(w, frame, valid):
+        parts = []
+        for parity in range(2):
+            re, im = w[parity][:128], w[parity][128:]
             residue = re * re + im * im - sorted_ref[frame, parity]
-            return above(residue * re, residue * im)
-
-        u0 = table_times(tables, 0, weighted(w0, 0))
-        u1 = table_times(tables, 2, weighted(w1, 1))
-        top, bottom = u0 + u1, u0 - u1
+            residue = jnp.where(valid, residue, jnp.zeros_like(residue))
+            parts.append(table_times(tables, 2 * parity, above(residue * re, residue * im)))
+        return parts
+
+    def across_back(u):
+        top, bottom = u[0] + u[1], u[0] - u[1]
         z_re = above(top[:128], bottom[:128])
         z_im = above(top[128:], bottom[128:])
         v0 = times_table(beside(z_re[:, :128], z_im[:, :128]), tables, 4)
         v1 = times_table(beside(z_re[:, 128:], z_im[:, 128:]), tables, 6)
-        back_re = [v0[:, :128] + v1[:, :128], v0[:, :128] - v1[:, :128]]
-        back_im = [v0[:, 128:] + v1[:, 128:], v0[:, 128:] - v1[:, 128:]]
-
+        return ([v0[:, :128] + v1[:, :128], v0[:, :128] - v1[:, :128]],
+                [v0[:, 128:] + v1[:, 128:], v0[:, 128:] - v1[:, 128:]])
+
+    def add_probe_terms(windows, backs):
         for b in range(2):
             at = slice(b * 128, b * 128 + 128)
-            probe_grad_ref[0, :, at] += window[0][b] * back_re[b] + window[1][b] * back_im[b]
-            probe_grad_ref[1, :, at] += window[0][b] * back_im[b] - window[1][b] * back_re[b]
+            re, im = probe_grad_ref[0, :, at], probe_grad_ref[1, :, at]
+            for window, (back_re, back_im) in zip(windows, backs):
+                re = re + (window[0][b] * back_re[b] + window[1][b] * back_im[b])
+                im = im + (window[0][b] * back_im[b] - window[1][b] * back_re[b])
+            probe_grad_ref[0, :, at] = re
+            probe_grad_ref[1, :, at] = im
+
+    def add_object_terms(place, back):
+        block0, shift, rows = place
+        back_re, back_im = back
+        probe = load_probe()
         before = lanes < shift
         zero = jnp.zeros((256, 128), F32)
         for channel in range(2):
@@ -439,9 +458,28 @@
             for block in range(3):
                 at = (channel, block0 + block, rows, slice(None))
                 grad_ref[at] = grad_ref[at] + adds[block]
+
+    last = positions_ref.shape[1] - 1
+
+    def add_pair(pair, carry):
+        slots = [start + pair * 2 + k for k in range(2)]
+        valid = [slot < end for slot in slots]
+        slots = [jnp.minimum(slot, last) for slot in slots]
+        windows, places = [], []
+        for slot in slots:
+            window, *spot = load_window(slot)
+            windows.append(window)
+            places.append(spot)
+        y = [across(window) for window in windows]
+        w = [along(each) for each in y]
+        u = [along_back(w[k], slots[k], valid[k]) for k in range(2)]
+        backs = [across_back(each) for each in u]
+        add_probe_terms(windows, backs)
+        for k in range(2):
+            add_object_terms(places[k], backs[k])
         return carry
 
-    lax.fori_loop(start, end, add_frame, 0)
+    lax.fori_loop(0, (end - start + 1) // 2, add_pair, 0)
 
 
 def frames(batch, counts, first, positions, ext, probe, ordered, tables):
@@ -732,6 +770,9 @@
     pass_on(1, 0)
     update(4)
     reduce.to_z()
+    late = down_way.stops[3]
+    on_time = jnp.logical_not(late)
+    pl.when(late)(reduce.from_z)
     join(0)
     join(1)
     pass_on(2, 0)
@@ -742,29 +783,32 @@
     pass_on(1, 1)
     if refetch:
         update(0)
-        reduce.from_z()
+        pl.when(late)(reduce.from_plane)
+        pl.when(on_time)(reduce.from_z)
         update(1)
         pass_on(2, 1)
         pass_on(3, 1)
         forward(0)
         update(2)
-        pass_up(0)
         forward(1)
         update(3)
         update(5)
+        pl.when(on_time)(reduce.from_plane)
+        pass_up(0)
         pass_up(1)
-        reduce.from_plane()
-        for index in (2, 3):
-            forward(index)
-            pass_up(index)
+        forward(2)
+        forward(3)
+        pass_up(2)
+        pass_up(3)
     else:
         update(5)
-        reduce.from_z()
+        pl.when(on_time)(reduce.from_z)
+        pl.when(late)(reduce.from_plane)
         pass_on(2, 1)
         pass_on(3, 1)
         update(0)
         update(1)
-        reduce.from_plane()
+        pl.when(on_time)(reduce.from_plane)
         update(2)
         update(3)
     reduce.end()

time: 140 us -> 137 us (0.979); the launches traced: 140 us -> 139 us
    pallas_call x2, Pallas kernels: 7.31 us -> 4.22 us  [frames(): pl.pallas_call(functools.partial(frames_kernel, batch), name=f'frames{bat...]
    pallas_call x2, Pallas kernels: 105 us -> 107 us  [exchange(): pl.pallas_call(functools.partial(exchange_kernel, refetch), name=f'exchan...]
where the time goes in v3:
time: 137 us; the launch traced here: 139 us
  Pallas kernels  134 us (98%)
  local copies, waits for them, and re-layouts  2.72 us (2%)
  between operations  2.13 us (2%)
    pallas_call x2, Pallas kernels, exchange(): pl.pallas_call(functools.partial(exchange_kernel, refetch), name=f'exchan...  107 us
    pallas_call x1, Pallas kernels, fetch(): pl.pallas_call(fetch_kernel, name='fetch', out_shape=(jax.ShapeDtypeStruc...  22.6 us
    pallas_call x2, Pallas kernels, frames(): pl.pallas_call(functools.partial(frames_kernel, batch), name=f'frames{bat...  4.22 us

profile of v3, /device:TPU:1, one launch (start us, length us, event | category | flops | bytes accessed | tf_op | source)
XLA Modules:
  0.0 138.8 jit_solution(15964478533287313913)
XLA Ops:
  0.6 0.0 copy-start
  0.6 0.0 copy-start.1
  2.1 0.0 copy-start.2
  2.1 0.9 copy-done.2
  3.0 0.0 copy-start.3
  3.0 22.6 %fetch.1 = (f32[2,5,640,128]{3,2,1,0:T(8,128)S(1)}, f32[8,2,128,256]{3,2,1,0:T(8,128)S(1)}) custom-call(f32[2,384,384]{2,1,0:T(8,128)} %object_ref.1, f32[8,256,256]{2,1,0:T(8,128)} %bitcast.6, bf16[256,256]{1,0:T(8,128)(2,1)S(1)} %copy-done.2), custom_call_target="tpu_custom_call" | custom-call | tf_op jit(solution)/shard_map/fetch/pallas_call | solution.py:322
  25.6 0.0 copy-done
  25.6 0.0 copy-done.1
  25.6 0.0 copy-done.3
  25.6 3.4 %frames0.1 = (f32[2,5,640,128]{3,2,1,0:T(8,128)S(1)}, f32[2,256,256]{2,1,0:T(8,128)S(1)}) custom-call(s32[1,1]{1,0:T(1,128)S(6)} %copy.12.counts_ref, s32[1,1]{1,0:T(1,128)S(6)} %copy.13.first_ref, s32[2,8]{1,0:T(2,128)S(1)} %bitcast.4, f32[2,5,640,128]{3,2,1,0:T(8,128)S(1)} %get-tuple-element.10.ext_ref.object_ref, f32[2,256,256]{2,1,0:T(8,128)S(1)} %copy-done.1, ...), custom_call_target="tpu_custom_call" | custom-call | tf_op jit(solution)/shard_map/frames0/pallas_call | solution.py:486
  29.1 49.8 %exchange1.1 = (f32[2,5,640,128]{3,2,1,0:T(8,128)S(1)}, f32[2,256,256]{2,1,0:T(8,128)S(1)}) custom-call(f32[2,5,640,128]{3,2,1,0:T(8,128)S(1)} %get-tuple-element.10.ext_ref.object_ref, f32[2,5,640,128]{3,2,1,0:T(8,128)S(1)} %get-tuple-element.12.grad_ref, f32[2,256,256]{2,1,0:T(8,128)S(1)} %copy-done.1, f32[2,256,256]{2,1,0:T(8,128)S(1)} %get-tuple-element.13.probe_grad_ref), custom_call_target="tpu_custom_call" | custom-call | tf_op jit(solution)/shard_map/exchange1/pallas_call | solution.py:841
  78.9 0.8 frames1.1
  79.7 57.3 %exchange0.1 = (f32[2,384,384]{2,1,0:T(8,128)S(1)}, f32[2,256,256]{2,1,0:T(8,128)S(1)}) custom-call(f32[2,5,640,128]{3,2,1,0:T(8,128)S(1)} %get-tuple-element.14.ext_ref.object_ref, f32[2,5,640,128]{3,2,1,0:T(8,128)S(1)} %get-tuple-element.16.grad_ref, f32[2,256,256]{2,1,0:T(8,128)S(1)} %get-tuple-element.15.probe_ref, ...), custom_call_target="tpu_custom_call" | custom-call | tf_op jit(solution)/shard_map/exchange0/pallas_call | solution.py:841
  137.0 1.0 copy.14
  138.0 0.8 copy.15
Async XLA Ops:
  0.6 25.0 %copy-start = (bf16[8,256,256]{2,1,0:T(8,128)(2,1)S(1)}, bf16[8,256,256]{2,1,0:T(8,128)(2,1)}, u32[]{:S(2)}) copy-start(bf16[8,256,256]{2,1,0:T(8,128)(2,1)} %constant.4.clone.tables) | copy-start | bytes 3145732
  0.6 25.0 %copy-start.1 = (f32[2,256,256]{2,1,0:T(8,128)S(1)}, f32[2,256,256]{2,1,0:T(8,128)}, u32[]{:S(2)}) copy-start(f32[2,256,256]{2,1,0:T(8,128)} %probe_ref.3) | copy-start | bytes 1572868
  2.1 0.9 copy-start.2
  3.0 22.7 %copy-start.3 = (s32[1,1,8,2]{2,3,1,0:T(2,128)S(1)}, s32[1,1,8,2]{2,3,1,0:T(2,128)}, u32[]{:S(2)}) copy-start(s32[1,1,8,2]{2,3,1,0:T(2,128)} %param.11) | copy-start | bytes 196

commit v4 on v3

--- a/solution.py
+++ b/solution.py
@@ -76,11 +76,8 @@
 class Detour:
     def __init__(self, paths, row, col):
         self.paths, self.row, self.col = paths, row, col
-        self.first = [is_at(row, col, paths[0][stop]) for stop in range(4)]
-        self.stops = [
-            functools.reduce(jnp.logical_or, [is_at(row, col, path[stop]) for path in paths])
-            for stop in range(4)
-        ]
+        self.each = [[is_at(row, col, path[stop]) for stop in range(4)] for path in paths]
+        self.stops = [functools.reduce(jnp.logical_or, marks) for marks in zip(*self.each)]
 
     def next_place(self, hop):
         row, col = place_of(self.paths[0][hop + 1])
@@ -615,7 +612,7 @@
         up_way.greet(barrier)
     for device in reduce.peers():
         pl.semaphore_signal(barrier, inc=1, device_id=device, device_id_type=MESH)
-    stops = (down_way.first, down_way.stops)
+    stops = (down_way.each[0], down_way.each[-1])
     sends_down, takes_above = row < N_ROW - 1, row > 0
     sends_right, takes_left = col < N_COL - 1, col > 0
     if refetch:
@@ -782,8 +779,8 @@
     pass_on(0, 1)
     pass_on(1, 1)
     if refetch:
+        pl.when(late)(reduce.from_plane)
         update(0)
-        pl.when(late)(reduce.from_plane)
         pl.when(on_time)(reduce.from_z)
         update(1)
         pass_on(2, 1)

time: 137 us -> 136 us (level); the launches traced: 139 us -> 134 us
  Pallas kernels: 134 us -> 129 us
    pallas_call x2, Pallas kernels: 107 us -> 94.4 us  [exchange(): pl.pallas_call(functools.partial(exchange_kernel, refetch), name=f'exchan...]
    pallas_call x2, Pallas kernels: 4.22 us -> 12.2 us  [frames(): pl.pallas_call(functools.partial(frames_kernel, batch), name=f'frames{bat...]
where the time goes in v4:
time: 136 us; the launch traced here: 134 us
  Pallas kernels  129 us (95%)
  local copies, waits for them, and re-layouts  2.72 us (2%)
  between operations  2.13 us (2%)
    pallas_call x2, Pallas kernels, exchange(): pl.pallas_call(functools.partial(exchange_kernel, refetch), name=f'exchan...  94.4 us
    pallas_call x1, Pallas kernels, fetch(): pl.pallas_call(fetch_kernel, name='fetch', out_shape=(jax.ShapeDtypeStruc...  22.6 us
    pallas_call x2, Pallas kernels, frames(): pl.pallas_call(functools.partial(frames_kernel, batch), name=f'frames{bat...  12.2 us
    unnamed x10, local copies, waits for them, and re-layouts  2.72 us

profile of v4, /device:TPU:1, one launch (start us, length us, event | category | flops | bytes accessed | tf_op | source)
XLA Modules:
  0.0 134.0 jit_solution(2557856802164116071)
XLA Ops:
  0.6 0.0 copy-start
  0.6 0.0 copy-start.1
  2.1 0.0 copy-start.2
  2.1 0.9 copy-done.2
  3.0 0.0 copy-start.3
  3.0 22.6 %fetch.1 = (f32[2,5,640,128]{3,2,1,0:T(8,128)S(1)}, f32[8,2,128,256]{3,2,1,0:T(8,128)S(1)}) custom-call(f32[2,384,384]{2,1,0:T(8,128)} %object_ref.1, f32[8,256,256]{2,1,0:T(8,128)} %bitcast.6, bf16[256,256]{1,0:T(8,128)(2,1)S(1)} %copy-done.2), custom_call_target="tpu_custom_call" | custom-call | tf_op jit(solution)/shard_map/fetch/pallas_call | solution.py:319
  25.6 0.0 copy-done
  25.6 0.0 copy-done.1
  25.6 0.0 copy-done.3
  25.6 6.1 %frames0.1 = (f32[2,5,640,128]{3,2,1,0:T(8,128)S(1)}, f32[2,256,256]{2,1,0:T(8,128)S(1)}) custom-call(s32[1,1]{1,0:T(1,128)S(6)} %copy.12.counts_ref, s32[1,1]{1,0:T(1,128)S(6)} %copy.13.first_ref, s32[2,8]{1,0:T(2,128)S(1)} %bitcast.4, f32[2,5,640,128]{3,2,1,0:T(8,128)S(1)} %get-tuple-element.10.ext_ref.object_ref, f32[2,256,256]{2,1,0:T(8,128)S(1)} %copy-done.1, ...), custom_call_target="tpu_custom_call" | custom-call | tf_op jit(solution)/shard_map/frames0/pallas_call | solution.py:483
  31.7 47.1 %exchange1.1 = (f32[2,5,640,128]{3,2,1,0:T(8,128)S(1)}, f32[2,256,256]{2,1,0:T(8,128)S(1)}) custom-call(f32[2,5,640,128]{3,2,1,0:T(8,128)S(1)} %get-tuple-element.10.ext_ref.object_ref, f32[2,5,640,128]{3,2,1,0:T(8,128)S(1)} %get-tuple-element.12.grad_ref, f32[2,256,256]{2,1,0:T(8,128)S(1)} %copy-done.1, f32[2,256,256]{2,1,0:T(8,128)S(1)} %get-tuple-element.13.probe_grad_ref), custom_call_target="tpu_custom_call" | custom-call | tf_op jit(solution)/shard_map/exchange1/pallas_call | solution.py:838
  78.8 6.1 %frames1.1 = (f32[2,5,640,128]{3,2,1,0:T(8,128)S(1)}, f32[2,256,256]{2,1,0:T(8,128)S(1)}) custom-call(s32[1,1]{1,0:T(1,128)S(6)} %copy.12.counts_ref, s32[1,1]{1,0:T(1,128)S(6)} %copy.13.first_ref, s32[2,8]{1,0:T(2,128)S(1)} %bitcast.5, f32[2,5,640,128]{3,2,1,0:T(8,128)S(1)} %get-tuple-element.14.ext_ref.object_ref, ...), custom_call_target="tpu_custom_call" | custom-call | tf_op jit(solution)/shard_map/frames1/pallas_call | solution.py:483
  84.9 47.3 %exchange0.1 = (f32[2,384,384]{2,1,0:T(8,128)S(1)}, f32[2,256,256]{2,1,0:T(8,128)S(1)}) custom-call(f32[2,5,640,128]{3,2,1,0:T(8,128)S(1)} %get-tuple-element.14.ext_ref.object_ref, f32[2,5,640,128]{3,2,1,0:T(8,128)S(1)} %get-tuple-element.16.grad_ref, f32[2,256,256]{2,1,0:T(8,128)S(1)} %get-tuple-element.15.probe_ref, ...), custom_call_target="tpu_custom_call" | custom-call | tf_op jit(solution)/shard_map/exchange0/pallas_call | solution.py:838
  132.2 1.0 copy.14
  133.3 0.8 copy.15
Async XLA Ops:
  0.6 25.0 %copy-start = (bf16[8,256,256]{2,1,0:T(8,128)(2,1)S(1)}, bf16[8,256,256]{2,1,0:T(8,128)(2,1)}, u32[]{:S(2)}) copy-start(bf16[8,256,256]{2,1,0:T(8,128)(2,1)} %constant.4.clone.tables) | copy-start | bytes 3145732
  0.6 25.0 %copy-start.1 = (f32[2,256,256]{2,1,0:T(8,128)S(1)}, f32[2,256,256]{2,1,0:T(8,128)}, u32[]{:S(2)}) copy-start(f32[2,256,256]{2,1,0:T(8,128)} %probe_ref.3) | copy-start | bytes 1572868
  2.1 0.9 copy-start.2
  3.0 22.7 %copy-start.3 = (s32[1,1,8,2]{2,3,1,0:T(2,128)S(1)}, s32[1,1,8,2]{2,3,1,0:T(2,128)}, u32[]{:S(2)}) copy-start(s32[1,1,8,2]{2,3,1,0:T(2,128)} %param.11) | copy-start | bytes 196
